TPU v7x, 512 devices: a 8x2x16 block of a 8x8x16 slice. The times are simulated.
512 devices in a mesh: cube: 2 (over y), gz: 128 (over x, z), gy: 2 (over core).
Axes of the slice: x: 8, y: 2, z: 16, core: 2. Of those that a mesh axis runs over, the one named last changes fastest.
The devices are a block of a 8x8x16 slice.
Arguments:
- noisy_cube: float32 [1024, 64, 256], P(('cube', 'gz'), 'gy'), parts along dimension 0, may hold values from -40 to 40
- thresholds: float32 [4], replicated, may hold values from 0.5 to 4
Outputs:
- denoised: float32 [1024, 4, 64, 256], P(('cube', 'gz'), None, 'gy'), parts along dimension 0
- gcv_score: float32 [8], P('cube'), parts along dimension 0
There are 2 independent parts, one for each index of `cube`. A program takes and returns all parts, laid end to end along the dimension named above; an argument that names none is the same for every part. Nothing has to cross between parts.
All inputs are finite; a program needn't handle non-finite values.
Results may differ from a plain program's by a relative error of at most 0.0003.
Values sent between devices are 32-bit elements; how exact they have to be, the bound alone decides.
A program may use at most 64 MiB of HBM per device.

v0:
```python
import functools

import jax
import jax.numpy as jnp
from jax import lax
from jax.sharding import Mesh
from jax.sharding import PartitionSpec as P

GZ = ("gz_0", "gz_1")
GZ_GY = ("gz_0", "gz_1", "gy")
CUBE_GZ = ("cube", "gz_0", "gz_1")


LOWPASS = (
    0.2303778133088964,
    0.7148465705529155,
    0.6308807679298587,
    -0.0279837694168599,
    -0.1870348117190931,
    0.0308413818355607,
    0.0328830116668852,
    -0.010597401785069,
)
HIGHPASS = tuple(((-1) ** tap_index * LOWPASS[7 - tap_index] for tap_index in range(8)))
lead_taps = 6
trail_taps = 3


def passed_along(array, axis, by):
    devices = lax.axis_size(axis)
    return lax.ppermute(array, axis, [(i, (i + by) % devices) for i in range(devices)])


def by_axis(array, axes):
    return functools.reduce(lax.psum, axes, array)


def analyse(extended, dimension_number, axis_length):
    lowband = 0.0
    highband = 0.0
    for tap_index in range(8):
        sliced = lax.slice_in_dim(
            extended, tap_index, tap_index + axis_length - 1, 2, dimension_number
        )
        lowband = lowband + LOWPASS[tap_index] * sliced
        highband = highband + HIGHPASS[tap_index] * sliced
    return (lowband, highband)


def synthesise(lowband, highband, dimension_number, axis_length):
    even_part = 0.0
    odd_part = 0.0
    for tap_index in range(4):
        low_slice = lax.slice_in_dim(
            lowband, 3 - tap_index, 3 - tap_index + axis_length, 1, dimension_number
        )
        high_slice = lax.slice_in_dim(
            highband, 3 - tap_index, 3 - tap_index + axis_length, 1, dimension_number
        )
        even_part = (
            even_part + LOWPASS[2 * tap_index] * low_slice + HIGHPASS[2 * tap_index] * high_slice
        )
        odd_part = (
            odd_part
            + LOWPASS[2 * tap_index + 1] * low_slice
            + HIGHPASS[2 * tap_index + 1] * high_slice
        )
    paired = jnp.stack([even_part, odd_part], dimension_number + 1)
    target = list(even_part.shape)
    target[dimension_number] = 2 * axis_length
    return paired.reshape(target)


def merge_bands(lowband, highband):
    stacked = jnp.stack([lowband, highband], 2)
    return stacked.reshape((lowband.shape[0], 2 * lowband.shape[1]) + lowband.shape[2:])


def split_bands(current):
    halves = current.reshape((current.shape[0], current.shape[1] // 2, 2) + current.shape[2:])
    return (halves[:, :, 0], halves[:, :, 1])


def wrap_ahead(input_tensor, dimension_number, border_extent):
    return jnp.concatenate(
        [input_tensor, lax.slice_in_dim(input_tensor, 0, border_extent, 1, dimension_number)],
        dimension_number,
    )


def wrap_behind(input_tensor, dimension_number, border_extent):
    axis_length = input_tensor.shape[dimension_number]
    return jnp.concatenate(
        [
            lax.slice_in_dim(
                input_tensor, axis_length - border_extent, axis_length, 1, dimension_number
            ),
            input_tensor,
        ],
        dimension_number,
    )


def z_shift(input_tensor, start_offset):
    return passed_along(input_tensor, GZ, start_offset)


def y_shift(input_tensor, start_offset):
    return passed_along(input_tensor, "gy", start_offset)


def raw_shift(input_tensor, start_offset):
    return passed_along(input_tensor, GZ, start_offset)


def following_panel(input_tensor, dimension_number, border_extent, holding_tensor):
    axis_length = input_tensor.shape[dimension_number]
    split_pieces = [input_tensor]
    covered = 0
    start_offset = 1
    while covered < border_extent:
        shift_amount = min(axis_length, border_extent - covered)
        split_pieces.append(
            holding_tensor(
                lax.slice_in_dim(input_tensor, 0, shift_amount, 1, dimension_number), -start_offset
            )
        )
        covered += shift_amount
        start_offset += 1
    return jnp.concatenate(split_pieces, dimension_number)


def preceding_panel(input_tensor, dimension_number, border_extent, holding_tensor):
    axis_length = input_tensor.shape[dimension_number]
    split_pieces = [input_tensor]
    covered = 0
    start_offset = 1
    while covered < border_extent:
        shift_amount = min(axis_length, border_extent - covered)
        split_pieces.insert(
            0,
            holding_tensor(
                lax.slice_in_dim(
                    input_tensor, axis_length - shift_amount, axis_length, 1, dimension_number
                ),
                start_offset,
            ),
        )
        covered += shift_amount
        start_offset += 1
    return jnp.concatenate(split_pieces, dimension_number)


def forward_level(volume):
    planes, number_of_lines, col_count = (volume.shape[0], volume.shape[2], volume.shape[3])
    lowband, highband = analyse(following_panel(volume, 0, lead_taps, z_shift), 0, planes)
    banded = merge_bands(lowband, highband)
    lowband, highband = analyse(following_panel(banded, 2, lead_taps, y_shift), 2, number_of_lines)
    banded = merge_bands(lowband, highband)
    lowband, highband = analyse(wrap_ahead(banded, 3, lead_taps), 3, col_count)
    return merge_bands(lowband, highband)


def synth_x(current):
    lowband, highband = split_bands(current)
    return synthesise(
        wrap_behind(lowband, 3, trail_taps),
        wrap_behind(highband, 3, trail_taps),
        3,
        current.shape[3],
    )


def synth_y(extended, number_of_lines):
    lowband, highband = split_bands(extended)
    return synthesise(lowband, highband, 2, number_of_lines)


def synth_z(extended, planes):
    lowband, highband = split_bands(extended)
    return synthesise(lowband, highband, 0, planes)


def inverse_level(coeffs):
    planes, number_of_lines = (coeffs.shape[0], coeffs.shape[2])
    current = synth_x(coeffs)
    current = synth_y(preceding_panel(current, 2, trail_taps, y_shift), number_of_lines)
    return synth_z(preceding_panel(current, 0, trail_taps, z_shift), planes)


def spread(details, approximation, limits):
    bounds = limits[None, :, None, None, None]
    widened = details[:, None]
    shrunk = widened - jnp.clip(widened, -bounds, bounds)
    complete = jnp.concatenate([approximation[:, :, None], shrunk], 2)
    return complete.reshape((complete.shape[0], complete.shape[1] * 8) + complete.shape[3:])


def raw_inverse(details, approximation, limits):
    planes, number_of_lines = (details.shape[0], details.shape[2])
    bundle = jnp.concatenate([details, approximation], 1)
    deeper = preceding_panel(bundle, 0, trail_taps, raw_shift)
    side_rows = passed_along(deeper[:, :, number_of_lines - trail_taps :], "gy", 1)
    extended = jnp.concatenate([side_rows, deeper], 2)
    band_count = details.shape[1]
    complete = spread(extended[:, :band_count], extended[:, band_count:], limits)
    current = synth_x(complete)
    current = synth_y(current, number_of_lines)
    return synth_z(current, planes)


def body(noisy_cube, thresholds):
    planes, number_of_lines, col_count = noisy_cube.shape
    level_one = forward_level(noisy_cube[:, None])
    level_two = forward_level(level_one[:, :1])
    details_one = level_one[:, 1:]
    details_two = level_two[:, 1:]
    squares = thresholds * thresholds
    square_grid = squares[:, None, None, None, None]
    bounds = thresholds[:, None, None, None, None]

    def weights(details):
        widened = details[None]
        return jnp.sum(square_grid / (square_grid + widened * widened), axis=(1, 2, 3, 4))

    def clipped(details):
        return jnp.sum(jnp.clip(details[None], -bounds, bounds) ** 2, axis=(1, 2, 3, 4))

    zero_local = weights(details_one) + weights(details_two)
    residual_local = clipped(details_one) + clipped(details_two)
    residual, zero_weight = (by_axis(residual_local, GZ_GY), by_axis(zero_local, GZ_GY))
    count_two = level_two.shape
    coarse_two = jnp.broadcast_to(
        level_two[:, :1], (count_two[0], thresholds.shape[0], count_two[2], count_two[3])
    )
    approximation = inverse_level(spread(details_two, coarse_two, thresholds))
    denoised = raw_inverse(details_one, approximation, thresholds)
    cell_count = planes * number_of_lines * col_count * lax.axis_size(GZ) * lax.axis_size("gy")
    gcv_score = cell_count * residual / (zero_weight * zero_weight)
    return (denoised, gcv_score)


def solution(mesh):
    split = Mesh(
        mesh.devices.reshape(mesh.shape["cube"], 8, 16, mesh.shape["gy"]),
        ("cube", "gz_0", "gz_1", "gy"),
    )
    placed = (P(CUBE_GZ, "gy", None), P())
    return jax.shard_map(
        body,
        mesh=split,
        in_specs=placed,
        out_specs=(P(CUBE_GZ, None, "gy", None), P("cube")),
        check_vma=False,
    )
```

profile of v0, /device:TPU:65, one launch (start us, length us, event | category | flops | bytes accessed | tf_op | source)
XLA Modules:
  0.0 217.4 jit_solution(8643480476871814956)
XLA Ops:
  0.6 47.8 %collective-permute-start = (f32[4,1,32,256]{3,2,0,1:T(8,128)}, f32[4,1,32,256]{3,2,0,1:T(8,128)S(1)}, u32[]{:S(2)}, u32[]{:S(2)}) collective-permute-start(f32[4,1,32,256]{3,2,0,1:T(8,128)} %bitcast.170), channel_id=1, source_target_pairs={{0,254},{2,0},{4,2},{6,4},{8,6},{10,8},{12,10},{14,12},{16,14},{18... | collective-permute-start | bytes 393224 | tf_op jit(solution)/shard_map/ppermute | solution.py:31
  48.5 0.9 slice_bitcast_fusion.9
  49.3 1.9 collective-permute-start.1
  51.3 4.1 %collective-permute-done.1 = f32[2,1,32,256]{3,2,0,1:T(8,128)S(1)} collective-permute-done((f32[2,1,32,256]{3,2,0,1:T(8,128)S(1)}, f32[2,1,32,256]{3,2,0,1:T(8,128)S(1)}, u32[]{:S(2)}, u32[]{:S(2)}) %collective-permute-start.1) | collective-permute-done | bytes 65568 | tf_op jit(solution)/shard_map/ppermute | solution.py:31
  55.4 0.9 pad_maximum_fusion.9
  56.3 1.0 add_bitcast_fusion.11
  57.3 3.9 %collective-permute-start.2 = (f32[2,2,6,256]{3,2,1,0:T(8,128)S(1)}, f32[2,2,6,256]{3,2,1,0:T(8,128)S(1)}, u32[]{:S(2)}, u32[]{:S(2)}) collective-permute-start(f32[2,2,6,256]{3,2,1,0:T(8,128)S(1)} %slice.533), channel_id=1, source_target_pairs={{0,1},{1,0},{2,3},{3,2},{4,5},{5,4},{6,7},{7,6},{8,9},{9,8},{10,11... | collective-permute-start | bytes 73736 | tf_op jit(solution)/shard_map/ppermute | solution.py:31
  61.4 0.6 collective-permute-done.2
  62.8 2.3 %slice.433 = f32[2,4,16,128]{3,2,1,0:T(8,128)S(1)} slice(f32[2,4,16,256]{3,2,1,0:T(8,128)S(1)} %bitcast.166), slice={[0:2:1], [0:4:1], [0:16:1], [1:256:2]} | slice | bytes 131072 | tf_op jit(solution)/shard_map/slice | solution.py:42
  65.1 2.3 %slice.432 = f32[2,4,16,128]{3,2,1,0:T(8,128)S(1)} slice(f32[2,4,16,256]{3,2,1,0:T(8,128)S(1)} %bitcast.167), slice={[0:2:1], [0:4:1], [0:16:1], [0:255:2]} | slice | bytes 131072 | tf_op jit(solution)/shard_map/slice | solution.py:42
  67.5 2.3 %slice.440 = f32[2,4,16,128]{3,2,1,0:T(8,128)S(1)} slice(f32[2,4,16,262]{3,2,1,0:T(8,128)S(1)} %pad_maximum_fusion.11), slice={[0:2:1], [0:4:1], [0:16:1], [7:262:2]} | slice | bytes 131072 | tf_op jit(solution)/shard_map/slice | solution.py:42
  69.8 2.3 %slice.439 = f32[2,4,16,128]{3,2,1,0:T(8,128)S(1)} slice(f32[2,4,16,262]{3,2,1,0:T(8,128)S(1)} %pad_maximum_fusion.11), slice={[0:2:1], [0:4:1], [0:16:1], [6:261:2]} | slice | bytes 131072 | tf_op jit(solution)/shard_map/slice | solution.py:42
  72.2 2.3 %slice.438 = f32[2,4,16,128]{3,2,1,0:T(8,128)S(1)} slice(f32[2,4,16,262]{3,2,1,0:T(8,128)S(1)} %pad_maximum_fusion.11), slice={[0:2:1], [0:4:1], [0:16:1], [5:260:2]} | slice | bytes 131072 | tf_op jit(solution)/shard_map/slice | solution.py:42
  74.5 2.3 %slice.437 = f32[2,4,16,128]{3,2,1,0:T(8,128)S(1)} slice(f32[2,4,16,262]{3,2,1,0:T(8,128)S(1)} %pad_maximum_fusion.11), slice={[0:2:1], [0:4:1], [0:16:1], [4:259:2]} | slice | bytes 131072 | tf_op jit(solution)/shard_map/slice | solution.py:42
  76.9 2.3 %slice.436 = f32[2,4,16,128]{3,2,1,0:T(8,128)S(1)} slice(f32[2,4,16,262]{3,2,1,0:T(8,128)S(1)} %pad_maximum_fusion.11), slice={[0:2:1], [0:4:1], [0:16:1], [3:258:2]} | slice | bytes 131072 | tf_op jit(solution)/shard_map/slice | solution.py:42
  79.2 2.3 %slice.435 = f32[2,4,16,128]{3,2,1,0:T(8,128)S(1)} slice(f32[2,4,16,262]{3,2,1,0:T(8,128)S(1)} %pad_maximum_fusion.11), slice={[0:2:1], [0:4:1], [0:16:1], [2:257:2]} | slice | bytes 131072 | tf_op jit(solution)/shard_map/slice | solution.py:42
  81.7 2.0 collective-permute-start.5
  83.6 5.7 %collective-permute-start.4 = (f32[2,1,16,128]{3,2,1,0:T(8,128)S(1)}, f32[2,1,16,128]{3,2,1,0:T(8,128)S(1)}, u32[]{:S(2)}, u32[]{:S(2)}) collective-permute-start(f32[2,1,16,128]{3,2,1,0:T(8,128)S(1)} %slice.538), channel_id=1, source_target_pairs={{0,252},{2,254},{4,0},{6,2},{8,4},{10,6},{12,8},{14,10},{16,12},{1... | collective-permute-start | bytes 49160 | tf_op jit(solution)/shard_map/ppermute | solution.py:31
  89.4 2.0 collective-permute-start.3
  91.4 1.2 collective-permute-done.4
  92.6 1.3 collective-permute-done.3
  93.9 3.7 %collective-permute-start.6 = (f32[1,2,6,128]{3,2,1,0:T(8,128)S(1)}, f32[1,2,6,128]{3,2,1,0:T(8,128)S(1)}, u32[]{:S(2)}, u32[]{:S(2)}) collective-permute-start(f32[1,2,6,128]{3,2,1,0:T(8,128)S(1)} %slice.545), channel_id=1, source_target_pairs={{0,1},{1,0},{2,3},{3,2},{4,5},{5,4},{6,7},{7,6},{8,9},{9,8},{10,11... | collective-permute-start | bytes 18440 | tf_op jit(solution)/shard_map/ppermute | solution.py:31
  98.0 0.5 collective-permute-done.6
  102.5 2.3 %collective-permute-start.7 = (f32[1,16,3,128]{1,2,3,0:T(4,128)S(1)}, f32[1,16,3,128]{1,2,3,0:T(4,128)S(1)}, u32[]{:S(2)}, u32[]{:S(2)}) collective-permute-start(f32[1,16,3,128]{1,2,3,0:T(4,128)S(1)} %slice.561), channel_id=1, source_target_pairs={{0,1},{1,0},{2,3},{3,2},{4,5},{5,4},{6,7},{7,6},{8,9},{9,8},{10,11... | collective-permute-start | bytes 73736 | tf_op jit(solution)/shard_map/ppermute | solution.py:31
  104.8 0.6 copy.177
  106.2 6.7 %collective-permute-start.10 = (f32[1,8,16,128]{3,1,2,0:T(8,128)S(1)}, f32[1,8,16,128]{3,1,2,0:T(8,128)S(1)}, u32[]{:S(2)}, u32[]{:S(2)}) collective-permute-start(f32[1,8,16,128]{3,1,2,0:T(8,128)S(1)} %bitcast.185), channel_id=1, source_target_pairs={{0,6},{2,8},{4,10},{6,12},{8,14},{10,16},{12,18},{14,20},{16,22},{... | collective-permute-start | bytes 196616 | tf_op jit(solution)/shard_map/ppermute | solution.py:31
  112.8 2.2 %collective-permute-start.9 = (f32[1,8,16,128]{3,1,2,0:T(8,128)S(1)}, f32[1,8,16,128]{3,1,2,0:T(8,128)S(1)}, u32[]{:S(2)}, u32[]{:S(2)}) collective-permute-start(f32[1,8,16,128]{3,1,2,0:T(8,128)S(1)} %bitcast.186), channel_id=1, source_target_pairs={{0,4},{2,6},{4,8},{6,10},{8,12},{10,14},{12,16},{14,18},{16,20},{1... | collective-permute-start | bytes 196616 | tf_op jit(solution)/shard_map/ppermute | solution.py:31
  115.1 2.8 %collective-permute-start.8 = (f32[1,8,16,128]{3,1,2,0:T(8,128)S(1)}, f32[1,8,16,128]{3,1,2,0:T(8,128)S(1)}, u32[]{:S(2)}, u32[]{:S(2)}) collective-permute-start(f32[1,8,16,128]{3,1,2,0:T(8,128)S(1)} %bitcast.187), channel_id=1, source_target_pairs={{0,2},{2,4},{4,6},{6,8},{8,10},{10,12},{12,14},{14,16},{16,18},{18... | collective-permute-start | bytes 196616 | tf_op jit(solution)/shard_map/ppermute | solution.py:31
  117.9 1.9 collective-permute-done.10
  119.9 3.3 %collective-permute-done.9 = f32[1,8,16,128]{3,1,2,0:T(8,128)S(1)} collective-permute-done((f32[1,8,16,128]{3,1,2,0:T(8,128)S(1)}, f32[1,8,16,128]{3,1,2,0:T(8,128)S(1)}, u32[]{:S(2)}, u32[]{:S(2)}) %collective-permute-start.9) | collective-permute-done | bytes 65568 | tf_op jit(solution)/shard_map/ppermute | solution.py:31
  123.3 2.1 collective-permute-done.8
  125.5 2.0 collective-permute-start.12
  127.5 2.0 collective-permute-start.11
  129.7 12.1 %all-reduce.1 = (f32[4]{0:T(128)S(1)}, f32[4]{0:T(128)S(1)}) all-reduce(f32[4]{0:T(128)S(1)} %add.989, f32[4]{0:T(128)S(1)} %add.984), channel_id=1, replica_groups=mesh['cube'=2,'gz_0'=8,'gz_1'=16,'gy'=2] {'gz_0'}, use_global_device_ids=true, to_apply=%region_7.8 | all-reduce | flops 8 | bytes 64 | tf_op jit(solution)/shard_map/psum | solution.py:35
  141.7 23.9 %all-reduce = (f32[4]{0:T(128)S(1)}, f32[4]{0:T(128)S(1)}) all-reduce(f32[4]{0:T(128)S(1)} %get-tuple-element.4, f32[4]{0:T(128)S(1)} %get-tuple-element.5), channel_id=1, replica_groups=mesh['cube'=2,'gz_0'=8,'gz_1'=16,'gy'=2] {'gz_1'}, use_global_device_ids=true, to_apply=%region_8.9 | all-reduce | flops 8 | bytes 64 | tf_op jit(solution)/shard_map/psum | solution.py:35
  165.6 14.5 %all-reduce.2 = (f32[4]{0:T(128)S(1)}, f32[4]{0:T(128)S(1)}) all-reduce(f32[4]{0:T(128)S(1)} %get-tuple-element.2, f32[4]{0:T(128)S(1)} %get-tuple-element.3), channel_id=1, replica_groups=mesh['cube'=2,'gz_0'=8,'gz_1'=16,'gy'=2] {'gy'}, use_global_device_ids=true, to_apply=%region_9.10 | all-reduce | flops 8 | bytes 64 | tf_op jit(solution)/shard_map/psum | solution.py:35
  180.1 2.5 %collective-permute-start.13 = (f32[5,11,3,128]{3,2,1,0:T(4,128)S(1)}, f32[5,11,3,128]{3,2,1,0:T(4,128)S(1)}, u32[]{:S(2)}, u32[]{:S(2)}) collective-permute-start(f32[5,11,3,128]{3,2,1,0:T(4,128)S(1)} %fusion.10), channel_id=1, source_target_pairs={{0,1},{1,0},{2,3},{3,2},{4,5},{5,4},{6,7},{7,6},{8,9},{9,8},{10,11... | collective-permute-start | bytes 253448 | tf_op jit(solution)/shard_map/ppermute | solution.py:31
  182.6 0.5 multiply_divide_fusion
  184.4 1.2 fusion.17
  186.2 3.8 %add_bitcast_fusion.1 = (f32[5,16,19,128,1]{3,1,2,0,4:T(8,128)S(1)}, f32[5,16,19,128,1]{3,1,2,0,4:T(8,128)S(1)}) fusion(f32[5,16,19,128]{3,1,2,0:T(8,128)S(1)} %bitcast.162, f32[5,16,19,128]{3,1,2,0:T(8,128)S(1)} %bitcast.160, f32[5,16,19,3]{3,1,2,0:T(8,128)S(1)} %slice.584, f32[5,16,19,3]{3,1,2,0:T(8,128)S(1)} %slice.587), kind=kLoop, calls=%fused_computation.19 | loop fusion | flops 7782400 | bytes 3149440 | tf_op jit(solution)/shard_map/stack | solution.py:68
  190.1 7.3 %copy.196 = f32[5,16,19,128,2]{2,4,3,1,0:T(2,128)} copy(f32[5,16,19,128,2]{3,1,2,0,4:T(8,128)S(1)} %pad_maximum_fusion.1) | data formatting | bytes 3112960 | tf_op jit(solution)/shard_map/stack | solution.py:68
  197.4 9.2 %fusion.16 = (f32[5,8,1,19,256]{3,4,2,1,0:T(8,128)}, f32[5,8,1,19,256]{3,4,2,1,0:T(8,128)}) fusion(f32[5,8,2,19,256]{3,4,2,1,0:T(8,128)} %bitcast.156), kind=kLoop, calls=%fused_computation.107 | loop fusion | bytes 3112960 | tf_op jit(solution)/shard_map/slice | solution.py:81
  206.5 3.3 %copy.228 = f32[5,8,1,19,256]{4,3,1,0,2:T(8,128)S(1)} copy(f32[5,8,1,19,256]{3,4,2,1,0:T(8,128)} %get-tuple-element.8) | data formatting | bytes 1556480
  209.8 3.3 %copy.229 = f32[5,8,1,19,256]{4,3,1,0,2:T(8,128)S(1)} copy(f32[5,8,1,19,256]{3,4,2,1,0:T(8,128)} %get-tuple-element.9) | data formatting | bytes 1556480
  213.2 0.9 add_bitcast_fusion.3
  214.2 1.1 copy.199
  215.3 0.9 reshape_reshape.15
  216.6 0.8 copy.209
  (101 shorter events, 8.8 us)
Async XLA Ops:
  0.6 60.5 %copy-start = (f32[4]{0:T(128)S(1)}, f32[4]{0:T(128)}, u32[]{:S(2)}) copy-start(f32[4]{0:T(128)} %param.3) | copy-start | bytes 52
  0.6 54.7 %collective-permute-start = (f32[4,1,32,256]{3,2,0,1:T(8,128)}, f32[4,1,32,256]{3,2,0,1:T(8,128)S(1)}, u32[]{:S(2)}, u32[]{:S(2)}) collective-permute-start(f32[4,1,32,256]{3,2,0,1:T(8,128)} %bitcast.170), channel_id=1, source_target_pairs={{0,254},{2,0},{4,2},{6,4},{8,6},{10,8},{12,10},{14,12},{16,14},{18... | collective-permute-start | bytes 393224 | tf_op jit(solution)/shard_map/ppermute | solution.py:31
  49.3 6.0 %collective-permute-start.1 = (f32[2,1,32,256]{3,2,0,1:T(8,128)S(1)}, f32[2,1,32,256]{3,2,0,1:T(8,128)S(1)}, u32[]{:S(2)}, u32[]{:S(2)}) collective-permute-start(f32[2,1,32,256]{3,2,0,1:T(8,128)S(1)} %slice_bitcast_fusion.9), channel_id=1, source_target_pairs={{0,252},{2,254},{4,0},{6,2},{8,4},{10,6},{12,8},{14,10},{16,12},{1... | collective-permute-start | bytes 196616 | tf_op jit(solution)/shard_map/ppermute | solution.py:31
  57.3 4.7 %collective-permute-start.2 = (f32[2,2,6,256]{3,2,1,0:T(8,128)S(1)}, f32[2,2,6,256]{3,2,1,0:T(8,128)S(1)}, u32[]{:S(2)}, u32[]{:S(2)}) collective-permute-start(f32[2,2,6,256]{3,2,1,0:T(8,128)S(1)} %slice.533), channel_id=1, source_target_pairs={{0,1},{1,0},{2,3},{3,2},{4,5},{5,4},{6,7},{7,6},{8,9},{9,8},{10,11... | collective-permute-start | bytes 73736 | tf_op jit(solution)/shard_map/ppermute | solution.py:31
  81.7 9.7 %collective-permute-start.5 = (f32[2,1,16,128]{3,2,1,0:T(8,128)S(1)}, f32[2,1,16,128]{3,2,1,0:T(8,128)S(1)}, u32[]{:S(2)}, u32[]{:S(2)}) collective-permute-start(f32[2,1,16,128]{3,2,1,0:T(8,128)S(1)} %slice.538), channel_id=1, source_target_pairs={{0,250},{2,252},{4,254},{6,0},{8,2},{10,4},{12,6},{14,8},{16,10},{... | collective-permute-start | bytes 49160 | tf_op jit(solution)/shard_map/ppermute | solution.py:31
  83.6 9.0 %collective-permute-start.4 = (f32[2,1,16,128]{3,2,1,0:T(8,128)S(1)}, f32[2,1,16,128]{3,2,1,0:T(8,128)S(1)}, u32[]{:S(2)}, u32[]{:S(2)}) collective-permute-start(f32[2,1,16,128]{3,2,1,0:T(8,128)S(1)} %slice.538), channel_id=1, source_target_pairs={{0,252},{2,254},{4,0},{6,2},{8,4},{10,6},{12,8},{14,10},{16,12},{1... | collective-permute-start | bytes 49160 | tf_op jit(solution)/shard_map/ppermute | solution.py:31
  89.4 4.5 %collective-permute-start.3 = (f32[2,1,16,128]{3,2,1,0:T(8,128)S(1)}, f32[2,1,16,128]{3,2,1,0:T(8,128)S(1)}, u32[]{:S(2)}, u32[]{:S(2)}) collective-permute-start(f32[2,1,16,128]{3,2,1,0:T(8,128)S(1)} %slice.538), channel_id=1, source_target_pairs={{0,254},{2,0},{4,2},{6,4},{8,6},{10,8},{12,10},{14,12},{16,14},{18... | collective-permute-start | bytes 49160 | tf_op jit(solution)/shard_map/ppermute | solution.py:31
  93.9 4.5 %collective-permute-start.6 = (f32[1,2,6,128]{3,2,1,0:T(8,128)S(1)}, f32[1,2,6,128]{3,2,1,0:T(8,128)S(1)}, u32[]{:S(2)}, u32[]{:S(2)}) collective-permute-start(f32[1,2,6,128]{3,2,1,0:T(8,128)S(1)} %slice.545), channel_id=1, source_target_pairs={{0,1},{1,0},{2,3},{3,2},{4,5},{5,4},{6,7},{7,6},{8,9},{9,8},{10,11... | collective-permute-start | bytes 18440 | tf_op jit(solution)/shard_map/ppermute | solution.py:31
  102.5 3.5 %collective-permute-start.7 = (f32[1,16,3,128]{1,2,3,0:T(4,128)S(1)}, f32[1,16,3,128]{1,2,3,0:T(4,128)S(1)}, u32[]{:S(2)}, u32[]{:S(2)}) collective-permute-start(f32[1,16,3,128]{1,2,3,0:T(4,128)S(1)} %slice.561), channel_id=1, source_target_pairs={{0,1},{1,0},{2,3},{3,2},{4,5},{5,4},{6,7},{7,6},{8,9},{9,8},{10,11... | collective-permute-start | bytes 73736 | tf_op jit(solution)/shard_map/ppermute | solution.py:31
  106.2 13.7 %collective-permute-start.10 = (f32[1,8,16,128]{3,1,2,0:T(8,128)S(1)}, f32[1,8,16,128]{3,1,2,0:T(8,128)S(1)}, u32[]{:S(2)}, u32[]{:S(2)}) collective-permute-start(f32[1,8,16,128]{3,1,2,0:T(8,128)S(1)} %bitcast.185), channel_id=1, source_target_pairs={{0,6},{2,8},{4,10},{6,12},{8,14},{10,16},{12,18},{14,20},{16,22},{... | collective-permute-start | bytes 196616 | tf_op jit(solution)/shard_map/ppermute | solution.py:31
  112.8 10.4 %collective-permute-start.9 = (f32[1,8,16,128]{3,1,2,0:T(8,128)S(1)}, f32[1,8,16,128]{3,1,2,0:T(8,128)S(1)}, u32[]{:S(2)}, u32[]{:S(2)}) collective-permute-start(f32[1,8,16,128]{3,1,2,0:T(8,128)S(1)} %bitcast.186), channel_id=1, source_target_pairs={{0,4},{2,6},{4,8},{6,10},{8,12},{10,14},{12,16},{14,18},{16,20},{1... | collective-permute-start | bytes 196616 | tf_op jit(solution)/shard_map/ppermute | solution.py:31
  115.1 10.3 %collective-permute-start.8 = (f32[1,8,16,128]{3,1,2,0:T(8,128)S(1)}, f32[1,8,16,128]{3,1,2,0:T(8,128)S(1)}, u32[]{:S(2)}, u32[]{:S(2)}) collective-permute-start(f32[1,8,16,128]{3,1,2,0:T(8,128)S(1)} %bitcast.187), channel_id=1, source_target_pairs={{0,2},{2,4},{4,6},{6,8},{8,10},{10,12},{12,14},{14,16},{16,18},{18... | collective-permute-start | bytes 196616 | tf_op jit(solution)/shard_map/ppermute | solution.py:31
  125.5 54.6 %collective-permute-start.12 = (f32[2,11,16,128]{3,2,1,0:T(8,128)S(1)}, f32[2,11,16,128]{3,2,1,0:T(8,128)S(1)}, u32[]{:S(2)}, u32[]{:S(2)}) collective-permute-start(f32[2,11,16,128]{3,2,1,0:T(8,128)S(1)} %pad_maximum_fusion.10), channel_id=1, source_target_pairs={{0,2},{2,4},{4,6},{6,8},{8,10},{10,12},{12,14},{14,16},{16,18},{18... | collective-permute-start | bytes 540680 | tf_op jit(solution)/shard_map/ppermute | solution.py:31
  127.5 52.6 %collective-permute-start.11 = (f32[1,11,16,128]{3,2,1,0:T(8,128)S(1)}, f32[1,11,16,128]{3,2,1,0:T(8,128)S(1)}, u32[]{:S(2)}, u32[]{:S(2)}) collective-permute-start(f32[1,11,16,128]{3,2,1,0:T(8,128)S(1)} %fusion.11), channel_id=1, source_target_pairs={{0,4},{2,6},{4,8},{6,10},{8,12},{10,14},{12,16},{14,18},{16,20},{1... | collective-permute-start | bytes 270344 | tf_op jit(solution)/shard_map/ppermute | solution.py:31
  180.1 3.2 %collective-permute-start.13 = (f32[5,11,3,128]{3,2,1,0:T(4,128)S(1)}, f32[5,11,3,128]{3,2,1,0:T(4,128)S(1)}, u32[]{:S(2)}, u32[]{:S(2)}) collective-permute-start(f32[5,11,3,128]{3,2,1,0:T(4,128)S(1)} %fusion.10), channel_id=1, source_target_pairs={{0,1},{1,0},{2,3},{3,2},{4,5},{5,4},{6,7},{7,6},{8,9},{9,8},{10,11... | collective-permute-start | bytes 253448 | tf_op jit(solution)/shard_map/ppermute | solution.py:31
where the time goes:
time: 218 us; the launch traced here: 217 us
  starting transfers between devices  87.4 us (40%)
  local copies, waits for them, and re-layouts  52.7 us (24%)
  blocking collectives  50.4 us (23%)
  waiting for transfers between devices  15.6 us (7%)
  other arithmetic  9.86 us (5%)
    ppermute x14, starting transfers between devices, passed_along(): lax.ppermute(array, axis, [(i, (i + by) % devices) for i in range(devices)])  87.4 us
    psum x3, blocking collectives, by_axis(): return functools.reduce(lax.psum, axes, array)  50.4 us
    slice x32, local copies, waits for them, and re-layouts, analyse(): lax.slice_in_dim(extended, tap_index, tap_index + axis_length - 1, 2, dim...  22.2 us
    ppermute x14, waiting for transfers between devices, passed_along(): lax.ppermute(array, axis, [(i, (i + by) % devices) for i in range(devices)])  15.6 us
    slice x2, local copies, waits for them, and re-layouts, split_bands(): return (halves[:, :, 0], halves[:, :, 1])  10.4 us
    another operation x5, local copies, waits for them, and re-layouts, synthesise(): paired = jnp.stack([even_part, odd_part], dimension_number + 1)  10.1 us
    unnamed x4, local copies, waits for them, and re-layouts  6.63 us
    another operation x9, other arithmetic, synthesise(): paired = jnp.stack([even_part, odd_part], dimension_number + 1)  5.39 us
  transfers between devices with their start and end apart: 14, of which 10 were waited for; matrix products, arithmetic and copies ran while one was open for 1% of the time, Pallas kernels for 0%

commit v1 on v0

v1 whole, which is shorter than its diff:
```python
import functools

import jax
import jax.numpy as jnp
import numpy as np
from jax import lax
from jax.experimental import pallas as pl
from jax.experimental.pallas import tpu as pltpu
from jax.sharding import Mesh
from jax.sharding import PartitionSpec as P

MESH = pl.DeviceIdType.MESH
CUBE_GZ = ("cube", "gz_0", "gz_1")

LOWPASS = (
    0.2303778133088964,
    0.7148465705529155,
    0.6308807679298587,
    -0.0279837694168599,
    -0.1870348117190931,
    0.0308413818355607,
    0.0328830116668852,
    -0.010597401785069,
)
HIGHPASS = tuple(((-1) ** tap * LOWPASS[7 - tap] for tap in range(8)))


def composed(second):
    taps = np.zeros(22)
    for outer in range(8):
        for inner in range(8):
            taps[2 * outer + inner] += second[outer] * LOWPASS[inner]
    return tuple(float(tap) for tap in taps)


DEEP_LOW = composed(LOWPASS)
DEEP_HIGH = composed(HIGHPASS)


def analysis_matrix(length):
    matrix = np.zeros((length, length))
    for k in range(length // 2):
        for tap in range(8):
            matrix[(2 * k + tap) % length, k] += LOWPASS[tap]
            matrix[(2 * k + tap) % length, length // 2 + k] += HIGHPASS[tap]
    return matrix


def in_two_parts(matrix):
    exact = matrix.astype(np.float32)
    upper = exact.astype(jnp.bfloat16)
    lower = (exact - upper.astype(np.float32)).astype(jnp.bfloat16)
    return np.stack([upper, lower])


def product(values, parts):
    upper = values.astype(jnp.bfloat16)
    lower = (values - upper.astype(jnp.float32)).astype(jnp.bfloat16)
    dot = functools.partial(jnp.dot, preferred_element_type=jnp.float32)
    return dot(upper, parts[0]) + (dot(lower, parts[0]) + dot(upper, parts[1]))


def weighted(taps, values):
    result = taps[0] * values[0]
    for tap, value in zip(taps[1:], values[1:]):
        result = result + tap * value
    return result


def synthesis_pair(low, high, odd):
    return weighted(LOWPASS[odd::2], low) + weighted(HIGHPASS[odd::2], high)


def shrunk(values, limit):
    return values - jnp.clip(values, -limit, limit)


def kernel(
    nx,
    nz,
    thr,
    x_hbm,
    a1_hbm,
    a1t_hbm,
    a2_hbm,
    a2t_hbm,
    den,
    gcv,
    raw,
    xa,
    ll,
    l2x,
    zb,
    lz,
    db,
    cb,
    zs2,
    co,
    cr,
    zs1,
    fo,
    a1,
    a1t,
    a2,
    a2t,
    row,
    tot,
    arx,
    arz,
    local_sem,
    send_sem,
    recv_sem,
    near_sem,
    mid_sem,
    far_sem,
):
    cube, gx, gz, gy = (lax.axis_index(n) for n in ("cube", "gz_0", "gz_1", "gy"))
    total = nx * nz
    flat = gx * nz + gz
    other = 1 - gy
    other_core = (cube, gx, gz, other)

    def along(offset):
        place = lax.rem(flat + (offset + total), total)
        return (cube, lax.div(place, nz), lax.rem(place, nz), gy)

    def across_x(offset, core):
        return (cube, lax.rem(gx + (offset + nx), nx), gz, core)

    def across_z(offset):
        return (cube, gx, lax.rem(gz + offset, nz), gy)

    sent = []

    def send(src, dst, device):
        index = len(sent)
        copy = pltpu.make_async_remote_copy(
            src_ref=src,
            dst_ref=dst,
            send_sem=send_sem.at[index],
            recv_sem=recv_sem.at[index],
            device_id=device,
            device_id_type=MESH,
        )
        copy.start()
        sent.append(copy)
        return copy

    def signal(sem, device):
        pl.semaphore_signal(sem, inc=1, device_id=device, device_id_type=MESH)

    loads = [pltpu.make_async_copy(x_hbm, raw.at[:, 0:32, :], local_sem.at[0])]
    for index, (src, dst) in enumerate(
        ((a1_hbm, a1), (a2_hbm, a2), (a2t_hbm, a2t), (a1t_hbm, a1t))
    ):
        loads.append(pltpu.make_async_copy(src, dst, local_sem.at[index + 1]))
    for load in loads:
        load.start()

    barrier = pltpu.get_barrier_semaphore()
    nearest = (along(1), along(-1), across_x(1, gy), across_x(-1, gy))
    for device in (other_core,) + nearest:
        signal(barrier, device)
    pl.semaphore_wait(barrier, 5)

    loads[0].wait()
    rows_copy = send(raw.at[:, 0:24, :], raw.at[:, 32:56, :], other_core)

    for device in nearest:
        signal(near_sem, device)
    pl.semaphore_wait(near_sem, 4)
    for device in (along(2), along(-2), across_x(2, gy), across_x(-2, gy)):
        signal(mid_sem, device)

    loads[1].wait()
    own = product(raw[:, 0:32, :].reshape(128, 256), a1)
    for sx in range(2):
        xa[sx, :, 0:32, :] = own[:, 128 * sx : 128 * sx + 128].reshape(4, 32, 128)
    rows_copy.wait_recv()
    beyond = product(raw[:, 32:56, :].reshape(96, 256), a1)
    for sx in range(2):
        xa[sx, :, 32:56, :] = beyond[:, 128 * sx : 128 * sx + 128].reshape(4, 24, 128)

    for z in range(4):
        for sx in range(2):
            taps = [xa[sx, z, pl.ds(j, 16, stride=2), :] for j in range(8)]
            low = weighted(LOWPASS, taps)
            zb[4 + z, sx] = low
            zb[4 + z, 2 + sx] = weighted(HIGHPASS, taps)
            if sx == 0:
                ll[z, 0:16, :] = low
                taps = [xa[sx, z, pl.ds(32 + j, 8, stride=2), :] for j in range(8)]
                ll[z, 16:24, :] = weighted(LOWPASS, taps)

    loads[2].wait()
    l2x[...] = product(ll[...].reshape(96, 128), a2).reshape(4, 24, 128)
    for z in range(4):
        taps = [l2x[z, pl.ds(j, 8, stride=2), :] for j in range(8)]
        lz[8 + z, 0] = weighted(LOWPASS, taps)
        lz[8 + z, 1] = weighted(HIGHPASS, taps)

    deep = lz.at[8:12]
    deep_copies = [
        send(deep, lz.at[0:4], along(2)),
        send(deep, lz.at[16:20], along(-2)),
        send(deep, lz.at[4:8], along(1)),
        send(deep, lz.at[12:16], along(-1)),
    ]
    pl.semaphore_wait(mid_sem, 4)
    deep_copies.append(send(lz.at[8:10], lz.at[20:22], along(-3)))
    for device in (along(4), along(-4), other_core):
        signal(far_sem, device)
    plane_copies = [
        send(zb.at[4:8], zb.at[0:4], along(1)),
        send(zb.at[4:6], zb.at[8:10], along(-1)),
    ]

    limits = [thr[t] for t in range(4)]
    squares = [limit * limit for limit in limits]
    lane = lax.broadcasted_iota(jnp.int32, (8, 128), 1)
    first_half = lane < 64
    zero = jnp.zeros((8, 128), jnp.float32)

    for copy in deep_copies:
        copy.wait_recv()
    for sy in range(2):
        planes = [lz[i, sy] for i in range(22)]
        cb[3, 0, sy, 8:16, :] = weighted(DEEP_LOW, planes)
        cb[3, 1, sy, 8:16, :] = weighted(DEEP_HIGH, planes)
    coeff_copies = [
        send(cb.at[3, :, :, 8:16, :], cb.at[3 - offset, :, :, 8:16, :], along(offset))
        for offset in (3, -2, 2, -1, 1)
    ]

    residual = [zero] * 4
    weight = [zero] * 4
    for sz in range(2):
        for sy in range(2):
            c = cb[3, sz, sy, 8:16, :]
            square = c * c
            for t in range(4):
                cut = jnp.clip(c, -limits[t], limits[t])
                kept = squares[t] / (squares[t] + square)
                cut = cut * cut
                if sz == 0 and sy == 0:
                    cut = jnp.where(first_half, zero, cut)
                    kept = jnp.where(first_half, zero, kept)
                residual[t] = residual[t] + cut
                weight[t] = weight[t] + kept

    for copy in plane_copies:
        copy.wait_recv()
    for band in range(4):
        for k in range(2):
            planes = [zb[2 * k + j, band] for j in range(8)]
            if band:
                db[1 + k, band - 1, 8:24, :] = weighted(LOWPASS, planes)
            db[1 + k, 3 + band, 8:24, :] = weighted(HIGHPASS, planes)
    detail_copies = [
        send(db.at[1:3, :, 8:24, :], db.at[3:5, :, 8:24, :], along(-1)),
        send(db.at[2, :, 8:24, :], db.at[0, :, 8:24, :], along(1)),
    ]

    def add_band(band, sums):
        sums = list(sums)
        for k in range(2):
            for part in range(2):
                c = db[1 + k, band, 8 + 8 * part : 16 + 8 * part, :]
                square = c * c
                for t in range(4):
                    cut = jnp.clip(c, -limits[t], limits[t])
                    sums[t] = sums[t] + cut * cut
                    sums[4 + t] = sums[4 + t] + squares[t] / (squares[t] + square)
        return tuple(sums)

    sums = lax.fori_loop(0, 7, add_band, tuple(residual + weight))

    def as_row(parts):
        line = jnp.zeros((1, 128), jnp.float32)
        for t, part in enumerate(parts):
            value = jnp.sum(jnp.sum(part, axis=0, keepdims=True), axis=1, keepdims=True)
            line = jnp.where(lane[0:1] == t, value, line)
        return line

    row[0:1, :] = as_row(sums[0:4])
    row[1:2, :] = as_row(sums[4:8])
    slot = gy * nx + gx
    arx[pl.ds(slot, 1)] = row[...].reshape(1, 2, 128)
    pl.semaphore_wait(far_sem, 3)
    x_copies = [
        send(row, arx.at[slot], across_x(offset, core))
        for core in (gy, other)
        for offset in range(nx)
        if not (core is gy and offset == 0)
    ]

    for copy in coeff_copies:
        copy.wait_recv()
    deep_rows = send(cb.at[:, :, :, 8:16, :], cb.at[:, :, :, 0:8, :], other_core)
    for copy in detail_copies:
        copy.wait_recv()
    detail_rows = send(db.at[:, :, 16:24, :], db.at[:, :, 0:8, :], other_core)

    for copy in x_copies:
        copy.wait_recv()
    tot[...] = jnp.sum(arx[...], axis=0)
    arz[pl.ds(gz, 1)] = tot[...].reshape(1, 2, 128)
    z_copies = [send(tot, arz.at[gz], across_z(offset)) for offset in range(1, nz)]

    deep_rows.wait_recv()

    def deep_along_z(t, carry):
        limit = thr[t]
        for sy in range(2):
            for part in range(2):
                bands = []
                for sz in range(2):
                    values = []
                    for m in range(6):
                        c = cb[m, sz, sy, 8 * part : 8 * part + 8, :]
                        s = shrunk(c, limit)
                        values.append(jnp.where(first_half, c, s) if sz + sy == 0 else s)
                    bands.append(values)
                for k in range(5):
                    p = 3 + (k + 1) // 2
                    odd = (k + 1) % 2
                    order = [p - i for i in range(4)]
                    zs2[t, k, sy, 8 + 8 * part : 16 + 8 * part, :] = synthesis_pair(
                        [bands[0][i] for i in order], [bands[1][i] for i in order], odd
                    )
        return carry

    lax.fori_loop(0, 4, deep_along_z, 0)

    def deep_along_y(t, carry):
        for k in range(5):
            low = [zs2[t, k, 0, 8 - i : 24 - i, :] for i in range(4)]
            high = [zs2[t, k, 1, 8 - i : 24 - i, :] for i in range(4)]
            co[t, k, pl.ds(0, 16, stride=2), :] = synthesis_pair(low, high, 0)
            co[t, k, pl.ds(1, 16, stride=2), :] = synthesis_pair(low, high, 1)
        return carry

    lax.fori_loop(0, 4, deep_along_y, 0)
    loads[3].wait()
    cr[...] = product(co[:, :, 8:32, :].reshape(480, 128), a2t).reshape(4, 5, 24, 128)

    detail_rows.wait_recv()

    def along_z(t, carry):
        limit = thr[t]
        for part in range(3):
            rows = slice(8 * part, 8 * part + 8)
            for band in range(4):
                if band:
                    low = [shrunk(db[k, band - 1, rows, :], limit) for k in range(5)]
                else:
                    low = [cr[t, k, rows, :] for k in range(5)]
                high = [shrunk(db[k, 3 + band, rows, :], limit) for k in range(5)]
                for e in range(2):
                    order = [3 + e - i for i in range(4)]
                    for odd in range(2):
                        zs1[2 * e + odd, t, band, rows, :] = synthesis_pair(
                            [low[i] for i in order], [high[i] for i in order], odd
                        )
        return carry

    lax.fori_loop(0, 4, along_z, 0)

    def along_y(t, carry):
        for z in range(4):
            for sx in range(2):
                low = [zs1[z, t, sx, 8 - i : 24 - i, :] for i in range(4)]
                high = [zs1[z, t, 2 + sx, 8 - i : 24 - i, :] for i in range(4)]
                fo[sx, z, t, pl.ds(0, 16, stride=2), :] = synthesis_pair(low, high, 0)
                fo[sx, z, t, pl.ds(1, 16, stride=2), :] = synthesis_pair(low, high, 1)
        return carry

    lax.fori_loop(0, 4, along_y, 0)
    loads[4].wait()
    both = jnp.concatenate([fo[0].reshape(512, 128), fo[1].reshape(512, 128)], axis=1)
    den[...] = product(both, a1t).reshape(4, 4, 32, 256)

    for copy in z_copies:
        copy.wait_recv()
    full = jnp.sum(arz[...], axis=0)
    cells = float(4 * 32 * 256 * total * 2)
    weights = jnp.where(lane[0:1] < 4, full[1:2], 1.0)
    gcv[...] = cells * full[0:1] / (weights * weights)
    for copy in sent:
        copy.wait_send()


def solution(mesh):
    nx, nz = 8, 16
    return on_grid(mesh, nx, nz)


def on_grid(mesh, nx, nz):
    split = Mesh(
        mesh.devices.reshape(mesh.shape["cube"], nx, nz, mesh.shape["gy"]),
        ("cube", "gz_0", "gz_1", "gy"),
    )
    full = in_two_parts(analysis_matrix(256))
    half = in_two_parts(analysis_matrix(128))
    matrices = (full, full.transpose(0, 2, 1), half, half.transpose(0, 2, 1))
    copies = 1 + 5 + 2 + 5 + 2 + (2 * nx - 1) + 2 + (nz - 1)
    f32 = jnp.float32

    def body(noisy_cube, thresholds):
        den, gcv = pl.pallas_call(
            functools.partial(kernel, nx, nz),
            out_shape=(
                jax.ShapeDtypeStruct((4, 4, 32, 256), f32),
                jax.ShapeDtypeStruct((1, 128), f32),
            ),
            in_specs=[pl.BlockSpec(memory_space=pltpu.SMEM)]
            + [pl.BlockSpec(memory_space=pl.ANY)] * 5,
            out_specs=(
                pl.BlockSpec(memory_space=pltpu.VMEM),
                pl.BlockSpec(memory_space=pltpu.VMEM),
            ),
            scratch_shapes=[
                pltpu.VMEM((4, 56, 256), f32),
                pltpu.VMEM((2, 4, 56, 128), f32),
                pltpu.VMEM((4, 24, 128), f32),
                pltpu.VMEM((4, 24, 128), f32),
                pltpu.VMEM((10, 4, 16, 128), f32),
                pltpu.VMEM((22, 2, 8, 128), f32),
                pltpu.VMEM((5, 7, 24, 128), f32),
                pltpu.VMEM((6, 2, 2, 16, 128), f32),
                pltpu.VMEM((4, 5, 2, 24, 128), f32),
                pltpu.VMEM((4, 5, 32, 128), f32),
                pltpu.VMEM((4, 5, 24, 128), f32),
                pltpu.VMEM((4, 4, 4, 24, 128), f32),
                pltpu.VMEM((2, 4, 4, 32, 128), f32),
                pltpu.VMEM((2, 256, 256), jnp.bfloat16),
                pltpu.VMEM((2, 256, 256), jnp.bfloat16),
                pltpu.VMEM((2, 128, 128), jnp.bfloat16),
                pltpu.VMEM((2, 128, 128), jnp.bfloat16),
                pltpu.VMEM((2, 128), f32),
                pltpu.VMEM((2, 128), f32),
                pltpu.VMEM((2 * nx, 2, 128), f32),
                pltpu.VMEM((nz, 2, 128), f32),
                pltpu.SemaphoreType.DMA((5,)),
                pltpu.SemaphoreType.DMA((copies,)),
                pltpu.SemaphoreType.DMA((copies,)),
                pltpu.SemaphoreType.REGULAR,
                pltpu.SemaphoreType.REGULAR,
                pltpu.SemaphoreType.REGULAR,
            ],
            compiler_params=pltpu.CompilerParams(collective_id=0, has_side_effects=True),
        )(thresholds, noisy_cube, *(jnp.asarray(m) for m in matrices))
        return den, gcv[0, 0:4]

    return jax.shard_map(
        body,
        mesh=split,
        in_specs=(P(CUBE_GZ, "gy", None), P()),
        out_specs=(P(CUBE_GZ, None, "gy", None), P("cube")),
        check_vma=False,
    )
```

time: 218 us -> 73 us (0.33)
  starting transfers between devices: 87.4 us -> 0 us
  Pallas kernels: 0 us -> 69.1 us
  blocking collectives: 50.4 us -> 0 us
  local copies, waits for them, and re-layouts: 52.7 us -> 3.05 us
  waiting for transfers between devices: 15.6 us -> 0 us
  other arithmetic: 9.86 us -> 0 us
    ppermute x14 -> x0, starting transfers between devices: 87.4 us -> none  [passed_along(): lax.ppermute(array, axis, [(i, (i + by) % devices) for i in range(devices)])]
    pallas_call x0 -> x1, Pallas kernels: none -> 69.1 us  [body(): pl.pallas_call(functools.partial(kernel, nx, nz), out_shape=(jax.ShapeDty...]
    psum x3 -> x0, blocking collectives: 50.4 us -> none  [by_axis(): return functools.reduce(lax.psum, axes, array)]
    slice x50 -> x0, local copies, waits for them, and re-layouts: 34.5 us -> none  [the longest x32 22.2 us: analyse(): lax.slice_in_dim(extended, tap_index, tap_index + axis_length - 1, 2, dim...]
    ppermute x14 -> x0, waiting for transfers between devices: 15.6 us -> none  [passed_along(): lax.ppermute(array, axis, [(i, (i + by) % devices) for i in range(devices)])]
    another operation x10 -> x0, local copies, waits for them, and re-layouts: 11 us -> none  [the longest x5 10.1 us: synthesise(): paired = jnp.stack([even_part, odd_part], dimension_number + 1)]
    another operation x19 -> x0, other arithmetic: 6.59 us -> none  [the longest x9 5.39 us: synthesise(): paired = jnp.stack([even_part, odd_part], dimension_number + 1)]
    unnamed x4 -> x3, local copies, waits for them, and re-layouts: 6.63 us -> 2.54 us
  transfers between devices with their start and end apart: 14 -> 0, of which waited for: 10 -> 0; matrix products, arithmetic and copies ran while one was open for 1% -> 0% of each run, Pallas kernels for 0% -> 0%
where the time goes in v1:
time: 73 us; the launch traced here: 72.8 us
  Pallas kernels  69.1 us (95%)
  local copies, waits for them, and re-layouts  3.05 us (4%)
    pallas_call x1, Pallas kernels, body(): pl.pallas_call(functools.partial(kernel, nx, nz), out_shape=(jax.ShapeDty...  69.1 us
    unnamed x3, local copies, waits for them, and re-layouts  2.54 us

profile of v1, /device:TPU:65, one launch (start us, length us, event | category | flops | bytes accessed | tf_op | source)
XLA Modules:
  0.0 72.8 jit_solution(2119365569642689914)
XLA Ops:
  0.6 69.1 %shard_map.77 = (f32[4,4,32,256]{3,2,1,0:T(8,128)}, f32[1,128]{1,0:T(1,128)}) custom-call(f32[4]{0:T(128)} %thr.1, f32[4,32,256]{2,1,0:T(8,128)} %x_hbm.1, bf16[2,256,256]{2,1,0:T(8,128)(2,1)} %constant.8.clone.a1_hbm, bf16[2,256,256]{2,1,0:T(8,128)(2,1)} %constant.9.clone.a1t_hbm, bf16[2,128,128]{2,1,0:T(8,128)(2,1)} %constant.10.clone.a2_hbm, ...), custom_call_target="tpu_custom_call" | custom-call | tf_op jit(solution)/shard_map/pallas_call | solution.py:410
  69.8 0.0 copy-start
  69.8 0.7 copy-done
  70.5 0.5 slice_bitcast_fusion
  71.0 1.9 %copy.9 = f32[4,4,32,256]{3,2,1,0:T(8,128)} copy(f32[4,4,32,256]{3,2,1,0:T(8,128)} %get-tuple-element.8) | data formatting | bytes 1048576
Async XLA Ops:
  69.8 0.7 copy-start

commit v2 on v1

v2 whole, which is shorter than its diff:
```python
import functools

import jax
import jax.numpy as jnp
import numpy as np
from jax import lax
from jax.experimental import pallas as pl
from jax.experimental.pallas import tpu as pltpu
from jax.sharding import Mesh
from jax.sharding import PartitionSpec as P

MESH = pl.DeviceIdType.MESH
CUBE_GZ = ("cube", "gz_0", "gz_1")

LOWPASS = (
    0.2303778133088964,
    0.7148465705529155,
    0.6308807679298587,
    -0.0279837694168599,
    -0.1870348117190931,
    0.0308413818355607,
    0.0328830116668852,
    -0.010597401785069,
)
HIGHPASS = tuple(((-1) ** tap * LOWPASS[7 - tap] for tap in range(8)))


def composed(second):
    taps = np.zeros(22)
    for outer in range(8):
        for inner in range(8):
            taps[2 * outer + inner] += second[outer] * LOWPASS[inner]
    return tuple(float(tap) for tap in taps)


DEEP_LOW = composed(LOWPASS)
DEEP_HIGH = composed(HIGHPASS)


def analysis_matrix(length):
    matrix = np.zeros((length, length))
    for k in range(length // 2):
        for tap in range(8):
            matrix[(2 * k + tap) % length, k] += LOWPASS[tap]
            matrix[(2 * k + tap) % length, length // 2 + k] += HIGHPASS[tap]
    return matrix


def in_two_parts(matrix):
    exact = matrix.astype(np.float32)
    upper = exact.astype(jnp.bfloat16)
    lower = (exact - upper.astype(np.float32)).astype(jnp.bfloat16)
    return np.stack([upper, lower])


def product(values, parts):
    upper = values.astype(jnp.bfloat16)
    lower = (values - upper.astype(jnp.float32)).astype(jnp.bfloat16)
    dot = functools.partial(jnp.dot, preferred_element_type=jnp.float32)
    return dot(upper, parts[0]) + (dot(lower, parts[0]) + dot(upper, parts[1]))


def weighted(taps, values):
    result = taps[0] * values[0]
    for tap, value in zip(taps[1:], values[1:]):
        result = result + tap * value
    return result


def synthesis_pair(low, high, odd):
    return weighted(LOWPASS[odd::2], low) + weighted(HIGHPASS[odd::2], high)


def shrunk(values, limit):
    return values - jnp.clip(values, -limit, limit)


def kernel(
    nx,
    nz,
    thr_hbm,
    x_hbm,
    a1_hbm,
    a1t_hbm,
    a2t_hbm,
    den,
    gcv,
    thr,
    raw,
    xa,
    za,
    zb,
    part_out,
    part_in,
    da,
    db,
    cb,
    zs2,
    co,
    cr,
    zs1,
    fo,
    a1,
    a1t,
    a2t,
    row,
    tot,
    arx,
    arz,
    local_sem,
    send_sem,
    recv_sem,
    ready,
):
    cube, gx, gz, gy = (lax.axis_index(n) for n in ("cube", "gz_0", "gz_1", "gy"))
    total = nx * nz
    flat = gx * nz + gz
    other = 1 - gy
    other_core = (cube, gx, gz, other)

    def along(offset):
        place = lax.rem(flat + (offset + total), total)
        return (cube, lax.div(place, nz), lax.rem(place, nz), gy)

    def across_x(offset, core):
        return (cube, lax.rem(gx + (offset + nx), nx), gz, core)

    def across_z(offset):
        return (cube, gx, lax.rem(gz + offset, nz), gy)

    sent = []

    def send(src, dst, device):
        index = len(sent)
        copy = pltpu.make_async_remote_copy(
            src_ref=src,
            dst_ref=dst,
            send_sem=send_sem.at[index],
            recv_sem=recv_sem.at[index],
            device_id=device,
            device_id_type=MESH,
        )
        copy.start()
        sent.append(copy)
        return copy

    def signal(sem, *devices):
        for device in devices:
            pl.semaphore_signal(sem, inc=1, device_id=device, device_id_type=MESH)

    near_z, mid_z, far_z, near_x, mid_x, core = (ready.at[i] for i in range(6))

    loads = [pltpu.make_async_copy(x_hbm, raw.at[:, 0:32, :], local_sem.at[0])]
    for index, (src, dst) in enumerate(
        ((a1_hbm, a1), (thr_hbm, thr), (a2t_hbm, a2t), (a1t_hbm, a1t))
    ):
        loads.append(pltpu.make_async_copy(src, dst, local_sem.at[index + 1]))
    for load in loads:
        load.start()

    barrier = pltpu.get_barrier_semaphore()
    signal(
        barrier, other_core, along(1), along(-1), across_x(1, gy), across_x(-1, gy)
    )
    pl.semaphore_wait(barrier, 5)

    loads[0].wait()
    rows_copy = send(raw.at[:, 0:24, :], raw.at[:, 32:56, :], other_core)
    signal(near_z, along(1), along(-1))
    signal(near_x, across_x(1, gy), across_x(-1, gy))

    loads[1].wait()
    own = product(raw[:, 0:32, :].reshape(128, 256), a1)
    for band in range(3):
        xa[band, :, 0:32, :] = own[:, 128 * band : 128 * band + 128].reshape(4, 32, 128)
    pl.semaphore_wait(near_z, 2)
    signal(mid_z, along(2), along(-2))
    rows_copy.wait_recv()
    beyond = product(raw[:, 32:56, :].reshape(96, 256), a1)
    for band in range(3):
        xa[band, :, 32:56, :] = beyond[:, 128 * band : 128 * band + 128].reshape(4, 24, 128)

    deep = []
    for z in range(4):
        taps = [xa[2, z, pl.ds(i, 8, stride=4), :] for i in range(22)]
        deep.append((weighted(DEEP_LOW, taps), weighted(DEEP_HIGH, taps)))

    def partial(sz, sy, offset):
        filter_taps = (DEEP_LOW, DEEP_HIGH)[sz]
        planes = [z for z in range(4) if z + 8 - 4 * offset < 22]
        return weighted(
            [filter_taps[z + 8 - 4 * offset] for z in planes], [deep[z][sy] for z in planes]
        )

    part_copies = []
    for index, offset in enumerate((2, -2, -3, 1, -1)):
        for sz in range(2):
            for sy in range(2):
                part_out[index, sz, sy] = partial(sz, sy, offset)
        if offset == -3:
            pl.semaphore_wait(mid_z, 2)
        part_copies.append(send(part_out.at[index], part_in.at[index], along(offset)))

    for z in range(4):
        for sx in range(2):
            taps = [xa[sx, z, pl.ds(j, 16, stride=2), :] for j in range(8)]
            za[4 + z, sx] = weighted(LOWPASS, taps)
            zb[2 + z, sx] = weighted(HIGHPASS, taps)
    plane_copies = [
        send(za.at[4:8], za.at[0:4], along(1)),
        send(zb.at[2:6], zb.at[6:10], along(-1)),
        send(zb.at[4:6], zb.at[0:2], along(1)),
        send(za.at[4:6], za.at[8:10], along(-1)),
    ]
    signal(far_z, along(4), along(-4))
    pl.semaphore_wait(near_x, 2)
    signal(mid_x, across_x(2, gy), across_x(-2, gy))

    lane = lax.broadcasted_iota(jnp.int32, (8, 128), 1)
    first_half = lane < 64
    zero = jnp.zeros((8, 128), jnp.float32)
    loads[2].wait()
    limits = [thr[t] for t in range(4)]
    squares = [limit * limit for limit in limits]

    for copy in part_copies:
        copy.wait_recv()
    residual = [zero] * 4
    weight = [zero] * 4
    for sz in range(2):
        for sy in range(2):
            c = partial(sz, sy, 0)
            for index in range(5):
                c = c + part_in[index, sz, sy]
            cb[3, sz, sy, 8:16, :] = c
    coeff_copies = [
        send(cb.at[3, :, :, 8:16, :], cb.at[3 - offset, :, :, 8:16, :], along(offset))
        for offset in (3, -2, 2, -1, 1)
    ]
    for sz in range(2):
        for sy in range(2):
            c = cb[3, sz, sy, 8:16, :]
            square = c * c
            for t in range(4):
                cut = jnp.clip(c, -limits[t], limits[t])
                kept = squares[t] / (squares[t] + square)
                cut = cut * cut
                if sz == 0 and sy == 0:
                    cut = jnp.where(first_half, zero, cut)
                    kept = jnp.where(first_half, zero, kept)
                residual[t] = residual[t] + cut
                weight[t] = weight[t] + kept
    pl.semaphore_wait(mid_x, 2)
    signal(core, other_core)

    for copy in plane_copies:
        copy.wait_recv()
    for k in range(2):
        for sx in range(2):
            planes = [za[2 * k + j, sx] for j in range(8)]
            if sx:
                da[1 + k, 1, 8:24, :] = weighted(LOWPASS, planes)
            da[1 + k, 2 * sx, 8:24, :] = weighted(HIGHPASS, planes)
            planes = [zb[2 * k + j, sx] for j in range(8)]
            db[2 + k, 2 * sx, 8:24, :] = weighted(LOWPASS, planes)
            db[2 + k, 2 * sx + 1, 8:24, :] = weighted(HIGHPASS, planes)
    detail_copies = [
        send(da.at[1:3, :, 8:24, :], da.at[3:5, :, 8:24, :], along(-1)),
        send(db.at[2:4, :, 8:24, :], db.at[0:2, :, 8:24, :], along(1)),
        send(db.at[2, :, 8:24, :], db.at[4, :, 8:24, :], along(-1)),
        send(da.at[2, :, 8:24, :], da.at[0, :, 8:24, :], along(1)),
    ]

    def add_bands(ref, first):
        def add_band(band, sums):
            sums = list(sums)
            for k in range(2):
                for half in range(2):
                    c = ref[first + k, band, 8 + 8 * half : 16 + 8 * half, :]
                    square = c * c
                    for t in range(4):
                        cut = jnp.clip(c, -limits[t], limits[t])
                        sums[t] = sums[t] + cut * cut
                        sums[4 + t] = sums[4 + t] + squares[t] / (squares[t] + square)
            return tuple(sums)

        return add_band

    sums = lax.fori_loop(0, 3, add_bands(da, 1), tuple(residual + weight))
    sums = lax.fori_loop(0, 4, add_bands(db, 2), sums)

    def as_row(parts):
        line = jnp.zeros((1, 128), jnp.float32)
        for t, part in enumerate(parts):
            value = jnp.sum(jnp.sum(part, axis=0, keepdims=True), axis=1, keepdims=True)
            line = jnp.where(lane[0:1] == t, value, line)
        return line

    row[0:1, :] = as_row(sums[0:4])
    row[1:2, :] = as_row(sums[4:8])
    slot = gy * nx + gx
    arx[pl.ds(slot, 1)] = row[...].reshape(1, 2, 128)
    pl.semaphore_wait(core, 1)
    pl.semaphore_wait(far_z, 2)
    x_copies = [
        send(row, arx.at[slot], across_x(offset, place))
        for offset in sorted(range(nx), key=lambda o: -min(o, nx - o))
        for place in (gy, other)
        if not (place is gy and offset == 0)
    ]

    for copy in detail_copies:
        copy.wait_recv()
    detail_rows = [
        send(da.at[:, :, 16:24, :], da.at[:, :, 0:8, :], other_core),
        send(db.at[:, :, 16:24, :], db.at[:, :, 0:8, :], other_core),
    ]

    for copy in detail_rows:
        copy.wait_recv()

    def along_z(t, carry):
        limit = thr[t]
        for part in range(3):
            rows = slice(8 * part, 8 * part + 8)

            def cut(ref, band):
                return [shrunk(ref[k, band, rows, :], limit) for k in range(5)]

            pairs = (
                (None, cut(da, 0)),
                (cut(da, 1), cut(da, 2)),
                (cut(db, 0), cut(db, 1)),
                (cut(db, 2), cut(db, 3)),
            )
            for band, (low, high) in enumerate(pairs):
                for e in range(2):
                    order = [3 + e - i for i in range(4)]
                    for odd in range(2):
                        value = weighted(HIGHPASS[odd::2], [high[i] for i in order])
                        if low is not None:
                            value = value + weighted(LOWPASS[odd::2], [low[i] for i in order])
                        zs1[2 * e + odd, t, band, rows, :] = value
        return carry

    lax.fori_loop(0, 4, along_z, 0)

    for copy in coeff_copies:
        copy.wait_recv()
    deep_rows = send(cb.at[:, :, :, 8:16, :], cb.at[:, :, :, 0:8, :], other_core)

    for copy in x_copies:
        copy.wait_recv()
    tot[...] = jnp.sum(arx[...], axis=0)
    arz[pl.ds(gz, 1)] = tot[...].reshape(1, 2, 128)
    z_copies = [
        send(tot, arz.at[gz], across_z(offset))
        for offset in sorted(range(1, nz), key=lambda o: min(o, nz - o))
    ]

    deep_rows.wait_recv()

    def deep_along_z(t, carry):
        limit = thr[t]
        for sy in range(2):
            for part in range(2):
                bands = []
                for sz in range(2):
                    values = []
                    for m in range(6):
                        c = cb[m, sz, sy, 8 * part : 8 * part + 8, :]
                        s = shrunk(c, limit)
                        values.append(jnp.where(first_half, c, s) if sz + sy == 0 else s)
                    bands.append(values)
                for k in range(5):
                    p = 3 + (k + 1) // 2
                    odd = (k + 1) % 2
                    order = [p - i for i in range(4)]
                    zs2[t, k, sy, 8 + 8 * part : 16 + 8 * part, :] = synthesis_pair(
                        [bands[0][i] for i in order], [bands[1][i] for i in order], odd
                    )
        return carry

    lax.fori_loop(0, 4, deep_along_z, 0)

    def deep_along_y(t, carry):
        for k in range(5):
            low = [zs2[t, k, 0, 8 - i : 24 - i, :] for i in range(4)]
            high = [zs2[t, k, 1, 8 - i : 24 - i, :] for i in range(4)]
            co[t, k, pl.ds(0, 16, stride=2), :] = synthesis_pair(low, high, 0)
            co[t, k, pl.ds(1, 16, stride=2), :] = synthesis_pair(low, high, 1)
        return carry

    lax.fori_loop(0, 4, deep_along_y, 0)
    loads[3].wait()
    cr[...] = product(co[:, :, 8:32, :].reshape(480, 128), a2t).reshape(4, 5, 24, 128)

    def along_y(t, carry):
        for part in range(3):
            rows = slice(8 * part, 8 * part + 8)
            low = [cr[t, k, rows, :] for k in range(5)]
            for e in range(2):
                order = [3 + e - i for i in range(4)]
                for odd in range(2):
                    zs1[2 * e + odd, t, 0, rows, :] = zs1[
                        2 * e + odd, t, 0, rows, :
                    ] + weighted(LOWPASS[odd::2], [low[i] for i in order])
        for z in range(4):
            for sx in range(2):
                low = [zs1[z, t, sx, 8 - i : 24 - i, :] for i in range(4)]
                high = [zs1[z, t, 2 + sx, 8 - i : 24 - i, :] for i in range(4)]
                fo[sx, z, t, pl.ds(0, 16, stride=2), :] = synthesis_pair(low, high, 0)
                fo[sx, z, t, pl.ds(1, 16, stride=2), :] = synthesis_pair(low, high, 1)
        return carry

    lax.fori_loop(0, 4, along_y, 0)
    loads[4].wait()
    both = jnp.concatenate([fo[0].reshape(512, 128), fo[1].reshape(512, 128)], axis=1)
    den[...] = product(both, a1t).reshape(4, 4, 32, 256)

    for copy in z_copies:
        copy.wait_recv()
    full = jnp.sum(arz[...], axis=0)
    cells = float(4 * 32 * 256 * total * 2)
    weights = jnp.where(lane[0:1] < 4, full[1:2], 1.0)
    gcv[...] = cells * full[0:1] / (weights * weights)
    for copy in sent:
        copy.wait_send()


def solution(mesh):
    nx, nz = 8, 16
    return on_grid(mesh, nx, nz)


def on_grid(mesh, nx, nz):
    split = Mesh(
        mesh.devices.reshape(mesh.shape["cube"], nx, nz, mesh.shape["gy"]),
        ("cube", "gz_0", "gz_1", "gy"),
    )
    first = analysis_matrix(256)
    second = analysis_matrix(128)
    forward = np.concatenate([first, first[:, 0:128] @ second], axis=1)
    matrices = [in_two_parts(m) for m in (forward, first.T, second.T)]
    copies = 1 + 5 + 4 + 5 + 4 + (2 * nx - 1) + 2 + 1 + (nz - 1)
    f32 = jnp.float32

    def body(noisy_cube, thresholds):
        den, gcv = pl.pallas_call(
            functools.partial(kernel, nx, nz),
            out_shape=(
                jax.ShapeDtypeStruct((4, 4, 32, 256), f32),
                jax.ShapeDtypeStruct((1, 128), f32),
            ),
            in_specs=[pl.BlockSpec(memory_space=pltpu.HBM)] * 5,
            out_specs=(
                pl.BlockSpec(memory_space=pltpu.VMEM),
                pl.BlockSpec(memory_space=pltpu.VMEM),
            ),
            scratch_shapes=[
                pltpu.SMEM((4,), f32),
                pltpu.VMEM((4, 56, 256), f32),
                pltpu.VMEM((3, 4, 56, 128), f32),
                pltpu.VMEM((10, 2, 16, 128), f32),
                pltpu.VMEM((10, 2, 16, 128), f32),
                pltpu.VMEM((5, 2, 2, 8, 128), f32),
                pltpu.VMEM((5, 2, 2, 8, 128), f32),
                pltpu.VMEM((5, 3, 24, 128), f32),
                pltpu.VMEM((5, 4, 24, 128), f32),
                pltpu.VMEM((6, 2, 2, 16, 128), f32),
                pltpu.VMEM((4, 5, 2, 24, 128), f32),
                pltpu.VMEM((4, 5, 32, 128), f32),
                pltpu.VMEM((4, 5, 24, 128), f32),
                pltpu.VMEM((4, 4, 4, 24, 128), f32),
                pltpu.VMEM((2, 4, 4, 32, 128), f32),
                pltpu.VMEM((2, 256, 384), jnp.bfloat16),
                pltpu.VMEM((2, 256, 256), jnp.bfloat16),
                pltpu.VMEM((2, 128, 128), jnp.bfloat16),
                pltpu.VMEM((2, 128), f32),
                pltpu.VMEM((2, 128), f32),
                pltpu.VMEM((2 * nx, 2, 128), f32),
                pltpu.VMEM((nz, 2, 128), f32),
                pltpu.SemaphoreType.DMA((5,)),
                pltpu.SemaphoreType.DMA((copies,)),
                pltpu.SemaphoreType.DMA((copies,)),
                pltpu.SemaphoreType.REGULAR((6,)),
            ],
            compiler_params=pltpu.CompilerParams(
                collective_id=0, has_side_effects=True, vmem_limit_bytes=12 * 1024 * 1024
            ),
        )(thresholds, noisy_cube, *(jnp.asarray(m) for m in matrices))
        return den, gcv[0, 0:4]

    return jax.shard_map(
        body,
        mesh=split,
        in_specs=(P(CUBE_GZ, "gy", None), P()),
        out_specs=(P(CUBE_GZ, None, "gy", None), P("cube")),
        check_vma=False,
    )
```

time: 73 us -> 74.9 us (1.026)
  local copies, waits for them, and re-layouts: 3.05 us -> 5.64 us
    unnamed x3 -> x11, local copies, waits for them, and re-layouts: 2.54 us -> 5.13 us
    pallas_call x1, Pallas kernels: 69.1 us -> 68.4 us  [body(): pl.pallas_call(functools.partial(kernel, nx, nz), out_shape=(jax.ShapeDty...]
where the time goes in v2:
time: 74.9 us; the launch traced here: 74.7 us
  Pallas kernels  68.4 us (91%)
  local copies, waits for them, and re-layouts  5.64 us (8%)
    pallas_call x1, Pallas kernels, body(): pl.pallas_call(functools.partial(kernel, nx, nz), out_shape=(jax.ShapeDty...  68.4 us
    unnamed x11, local copies, waits for them, and re-layouts  5.13 us

profile of v2, /device:TPU:65, one launch (start us, length us, event | category | flops | bytes accessed | tf_op | source)
XLA Modules:
  0.0 74.7 jit_solution(73412499408014136)
XLA Ops:
  0.6 0.0 copy-start
  0.6 1.0 %copy-done = bf16[2,256,384]{2,1,0:T(8,128)(2,1)S(1)} copy-done((bf16[2,256,384]{2,1,0:T(8,128)(2,1)S(1)}, bf16[2,256,384]{2,1,0:T(8,128)(2,1)}, u32[]{:S(2)}) %copy-start) | copy-done | bytes 393240
  1.6 0.0 copy-start.1
  1.6 0.9 %copy-done.1 = bf16[2,256,256]{2,1,0:T(8,128)(2,1)S(1)} copy-done((bf16[2,256,256]{2,1,0:T(8,128)(2,1)S(1)}, bf16[2,256,256]{2,1,0:T(8,128)(2,1)}, u32[]{:S(2)}) %copy-start.1) | copy-done | bytes 262168
  2.6 0.0 copy-start.2
  2.6 0.9 %copy-done.2 = f32[4,32,256]{2,1,0:T(8,128)S(1)} copy-done((f32[4,32,256]{2,1,0:T(8,128)S(1)}, f32[4,32,256]{2,1,0:T(8,128)}, u32[]{:S(2)}) %copy-start.2) | copy-done | bytes 131096
  3.5 0.0 copy-start.3
  3.5 0.8 %copy-done.3 = bf16[2,128,128]{2,1,0:T(8,128)(2,1)S(1)} copy-done((bf16[2,128,128]{2,1,0:T(8,128)(2,1)S(1)}, bf16[2,128,128]{2,1,0:T(8,128)(2,1)}, u32[]{:S(2)}) %copy-start.3) | copy-done | bytes 65560
  4.3 0.0 copy-start.4
  4.3 0.7 copy-done.4
  5.0 68.4 %shard_map.68 = (f32[4,4,32,256]{3,2,1,0:T(8,128)S(1)}, f32[1,128]{1,0:T(1,128)S(1)}) custom-call(f32[4]{0:T(128)S(1)} %copy-done.4, f32[4,32,256]{2,1,0:T(8,128)S(1)} %copy-done.2, bf16[2,256,384]{2,1,0:T(8,128)(2,1)S(1)} %copy-done, bf16[2,256,256]{2,1,0:T(8,128)(2,1)S(1)} %copy-done.1, bf16[2,128,128]{2,1,0:T(8,128)(2,1)S(1)} %copy-done.3), custom_call_target="tpu_custom_call" | custom-call | tf_op jit(solution)/shard_map/pallas_call | solution.py:449
  73.4 0.5 slice_bitcast_fusion
  73.9 0.8 %copy.8 = f32[4,4,32,256]{3,2,1,0:T(8,128)} copy(f32[4,4,32,256]{3,2,1,0:T(8,128)S(1)} %get-tuple-element.8) | data formatting | bytes 1048576
Async XLA Ops:
  0.6 1.0 %copy-start = (bf16[2,256,384]{2,1,0:T(8,128)(2,1)S(1)}, bf16[2,256,384]{2,1,0:T(8,128)(2,1)}, u32[]{:S(2)}) copy-start(bf16[2,256,384]{2,1,0:T(8,128)(2,1)} %constant.6.clone.a1_hbm) | copy-start | bytes 1179652
  1.6 0.9 %copy-start.1 = (bf16[2,256,256]{2,1,0:T(8,128)(2,1)S(1)}, bf16[2,256,256]{2,1,0:T(8,128)(2,1)}, u32[]{:S(2)}) copy-start(bf16[2,256,256]{2,1,0:T(8,128)(2,1)} %constant.7.clone.a1t_hbm) | copy-start | bytes 786436
  2.6 0.9 %copy-start.2 = (f32[4,32,256]{2,1,0:T(8,128)S(1)}, f32[4,32,256]{2,1,0:T(8,128)}, u32[]{:S(2)}) copy-start(f32[4,32,256]{2,1,0:T(8,128)} %x_hbm.1) | copy-start | bytes 393220
  3.5 0.8 %copy-start.3 = (bf16[2,128,128]{2,1,0:T(8,128)(2,1)S(1)}, bf16[2,128,128]{2,1,0:T(8,128)(2,1)}, u32[]{:S(2)}) copy-start(bf16[2,128,128]{2,1,0:T(8,128)(2,1)} %constant.8.clone.a2t_hbm) | copy-start | bytes 196612
  4.3 0.7 copy-start.4

commit v3 on v2

--- a/solution.py
+++ b/solution.py
@@ -88,11 +88,9 @@
     thr,
     raw,
     xa,
-    za,
-    zb,
+    zw,
     part_out,
     part_in,
-    da,
     db,
     cb,
     zs2,
@@ -110,7 +108,9 @@
     local_sem,
     send_sem,
     recv_sem,
-    ready,
+    link,
+    near,
+    mid,
 ):
     cube, gx, gz, gy = (lax.axis_index(n) for n in ("cube", "gz_0", "gz_1", "gy"))
     total = nx * nz
@@ -128,27 +128,34 @@
     def across_z(offset):
         return (cube, gx, lax.rem(gz + offset, nz), gy)
 
-    sent = []
-
-    def send(src, dst, device):
-        index = len(sent)
-        copy = pltpu.make_async_remote_copy(
-            src_ref=src,
-            dst_ref=dst,
-            send_sem=send_sem.at[index],
-            recv_sem=recv_sem.at[index],
-            device_id=device,
+    groups = []
+
+    def send_all(whole, *copies):
+        index = len(groups)
+        sems = (send_sem.at[index], recv_sem.at[index])
+        for src, dst, device in copies:
+            pltpu.make_async_remote_copy(
+                src_ref=src,
+                dst_ref=dst,
+                send_sem=sems[0],
+                recv_sem=sems[1],
+                device_id=device,
+                device_id_type=MESH,
+            ).start()
+        group = pltpu.make_async_remote_copy(
+            src_ref=whole,
+            dst_ref=whole,
+            send_sem=sems[0],
+            recv_sem=sems[1],
+            device_id=other_core,
             device_id_type=MESH,
         )
-        copy.start()
-        sent.append(copy)
-        return copy
+        groups.append(group)
+        return group
 
     def signal(sem, *devices):
         for device in devices:
             pl.semaphore_signal(sem, inc=1, device_id=device, device_id_type=MESH)
-
-    near_z, mid_z, far_z, near_x, mid_x, core = (ready.at[i] for i in range(6))
 
     loads = [pltpu.make_async_copy(x_hbm, raw.at[:, 0:32, :], local_sem.at[0])]
     for index, (src, dst) in enumerate(
@@ -159,22 +166,31 @@
         load.start()
 
     barrier = pltpu.get_barrier_semaphore()
-    signal(
-        barrier, other_core, along(1), along(-1), across_x(1, gy), across_x(-1, gy)
-    )
-    pl.semaphore_wait(barrier, 5)
+
+    @pl.when(gy == 0)
+    def _():
+        signal(barrier, other_core)
+
+    @pl.when(gy == 1)
+    def _():
+        pl.semaphore_wait(barrier, 1)
+        signal(link, other_core)
+
+    @pl.when(gy == 0)
+    def _():
+        pl.semaphore_wait(link, 1)
+        signal(barrier, *(along(offset) for offset in (1, -1, 2, -2, 3, -3)))
+        signal(barrier, across_x(1, gy), across_x(-1, gy))
 
     loads[0].wait()
-    rows_copy = send(raw.at[:, 0:24, :], raw.at[:, 32:56, :], other_core)
-    signal(near_z, along(1), along(-1))
-    signal(near_x, across_x(1, gy), across_x(-1, gy))
+    rows_copy = send_all(
+        raw.at[:, 0:24, :], (raw.at[:, 0:24, :], raw.at[:, 32:56, :], other_core)
+    )
 
     loads[1].wait()
     own = product(raw[:, 0:32, :].reshape(128, 256), a1)
     for band in range(3):
         xa[band, :, 0:32, :] = own[:, 128 * band : 128 * band + 128].reshape(4, 32, 128)
-    pl.semaphore_wait(near_z, 2)
-    signal(mid_z, along(2), along(-2))
     rows_copy.wait_recv()
     beyond = product(raw[:, 32:56, :].reshape(96, 256), a1)
     for band in range(3):
@@ -192,29 +208,55 @@
             [filter_taps[z + 8 - 4 * offset] for z in planes], [deep[z][sy] for z in planes]
         )
 
-    part_copies = []
-    for index, offset in enumerate((2, -2, -3, 1, -1)):
+    offsets = (2, -2, -3, 1, -1)
+    for index, offset in enumerate(offsets):
         for sz in range(2):
             for sy in range(2):
                 part_out[index, sz, sy] = partial(sz, sy, offset)
-        if offset == -3:
-            pl.semaphore_wait(mid_z, 2)
-        part_copies.append(send(part_out.at[index], part_in.at[index], along(offset)))
+
+    @pl.when(gy == 0)
+    def _():
+        pl.semaphore_wait(barrier, 8)
+        signal(link, other_core)
+
+    @pl.when(gy == 1)
+    def _():
+        pl.semaphore_wait(link, 1)
+
+    part_copies = send_all(
+        part_in,
+        *(
+            (part_out.at[index], part_in.at[index], along(offset))
+            for index, offset in enumerate(offsets)
+        ),
+    )
 
     for z in range(4):
         for sx in range(2):
             taps = [xa[sx, z, pl.ds(j, 16, stride=2), :] for j in range(8)]
-            za[4 + z, sx] = weighted(LOWPASS, taps)
-            zb[2 + z, sx] = weighted(HIGHPASS, taps)
-    plane_copies = [
-        send(za.at[4:8], za.at[0:4], along(1)),
-        send(zb.at[2:6], zb.at[6:10], along(-1)),
-        send(zb.at[4:6], zb.at[0:2], along(1)),
-        send(za.at[4:6], za.at[8:10], along(-1)),
-    ]
-    signal(far_z, along(4), along(-4))
-    pl.semaphore_wait(near_x, 2)
-    signal(mid_x, across_x(2, gy), across_x(-2, gy))
+            zw[6 + z, sx] = weighted(LOWPASS, taps)
+            zw[6 + z, 2 + sx] = weighted(HIGHPASS, taps)
+    six = zw.at[0:6]
+    plane_copies = send_all(
+        six,
+        (zw.at[6:10, 0:2], zw.at[2:6, 0:2], along(1)),
+        (zw.at[6:10, 2:4], zw.at[10:14, 2:4], along(-1)),
+        (zw.at[8:10, 2:4], zw.at[4:6, 2:4], along(1)),
+        (zw.at[6:8, 0:2], zw.at[10:12, 0:2], along(-1)),
+    )
+    more_copies = send_all(
+        six,
+        (zw.at[8:10], zw.at[0:2], along(2)),
+        (zw.at[6:8], zw.at[14:16], along(-2)),
+        (zw.at[6:8, 2:4], zw.at[2:4, 2:4], along(1)),
+        (zw.at[8:10, 0:2], zw.at[12:14, 0:2], along(-1)),
+    )
+
+    @pl.when(gy == 0)
+    def _():
+        signal(near, along(3), along(-3), across_x(1, gy), across_x(-1, gy))
+        pl.semaphore_wait(near, 4)
+        signal(mid, along(2), along(-2), across_x(2, gy), across_x(-2, gy))
 
     lane = lax.broadcasted_iota(jnp.int32, (8, 128), 1)
     first_half = lane < 64
@@ -223,8 +265,7 @@
     limits = [thr[t] for t in range(4)]
     squares = [limit * limit for limit in limits]
 
-    for copy in part_copies:
-        copy.wait_recv()
+    part_copies.wait_recv()
     residual = [zero] * 4
     weight = [zero] * 4
     for sz in range(2):
@@ -233,10 +274,13 @@
             for index in range(5):
                 c = c + part_in[index, sz, sy]
             cb[3, sz, sy, 8:16, :] = c
-    coeff_copies = [
-        send(cb.at[3, :, :, 8:16, :], cb.at[3 - offset, :, :, 8:16, :], along(offset))
-        for offset in (3, -2, 2, -1, 1)
-    ]
+    coeff_copies = send_all(
+        cb.at[0:5, :, :, 8:16, :],
+        *(
+            (cb.at[3, :, :, 8:16, :], cb.at[3 - offset, :, :, 8:16, :], along(offset))
+            for offset in (3, -2, 2, -1, 1)
+        ),
+    )
     for sz in range(2):
         for sy in range(2):
             c = cb[3, sz, sy, 8:16, :]
@@ -250,33 +294,26 @@
                     kept = jnp.where(first_half, zero, kept)
                 residual[t] = residual[t] + cut
                 weight[t] = weight[t] + kept
-    pl.semaphore_wait(mid_x, 2)
-    signal(core, other_core)
-
-    for copy in plane_copies:
-        copy.wait_recv()
+
+    def level_one(k, half):
+        for sx in range(2):
+            band = 2 * half + sx
+            planes = [zw[2 * k + j, band] for j in range(8)]
+            if band:
+                db[k, 2 * band - 1, 8:24, :] = weighted(LOWPASS, planes)
+            db[k, 2 * band, 8:24, :] = weighted(HIGHPASS, planes)
+
+    plane_copies.wait_recv()
     for k in range(2):
-        for sx in range(2):
-            planes = [za[2 * k + j, sx] for j in range(8)]
-            if sx:
-                da[1 + k, 1, 8:24, :] = weighted(LOWPASS, planes)
-            da[1 + k, 2 * sx, 8:24, :] = weighted(HIGHPASS, planes)
-            planes = [zb[2 * k + j, sx] for j in range(8)]
-            db[2 + k, 2 * sx, 8:24, :] = weighted(LOWPASS, planes)
-            db[2 + k, 2 * sx + 1, 8:24, :] = weighted(HIGHPASS, planes)
-    detail_copies = [
-        send(da.at[1:3, :, 8:24, :], da.at[3:5, :, 8:24, :], along(-1)),
-        send(db.at[2:4, :, 8:24, :], db.at[0:2, :, 8:24, :], along(1)),
-        send(db.at[2, :, 8:24, :], db.at[4, :, 8:24, :], along(-1)),
-        send(da.at[2, :, 8:24, :], da.at[0, :, 8:24, :], along(1)),
-    ]
-
-    def add_bands(ref, first):
+        level_one(1 + k, 0)
+        level_one(2 + k, 1)
+
+    def add_bands(first):
         def add_band(band, sums):
             sums = list(sums)
             for k in range(2):
                 for half in range(2):
-                    c = ref[first + k, band, 8 + 8 * half : 16 + 8 * half, :]
+                    c = db[first + k, band, 8 + 8 * half : 16 + 8 * half, :]
                     square = c * c
                     for t in range(4):
                         cut = jnp.clip(c, -limits[t], limits[t])
@@ -286,8 +323,8 @@
 
         return add_band
 
-    sums = lax.fori_loop(0, 3, add_bands(da, 1), tuple(residual + weight))
-    sums = lax.fori_loop(0, 4, add_bands(db, 2), sums)
+    sums = lax.fori_loop(0, 3, add_bands(1), tuple(residual + weight))
+    sums = lax.fori_loop(3, 7, add_bands(2), sums)
 
     def as_row(parts):
         line = jnp.zeros((1, 128), jnp.float32)
@@ -300,39 +337,46 @@
     row[1:2, :] = as_row(sums[4:8])
     slot = gy * nx + gx
     arx[pl.ds(slot, 1)] = row[...].reshape(1, 2, 128)
-    pl.semaphore_wait(core, 1)
-    pl.semaphore_wait(far_z, 2)
-    x_copies = [
-        send(row, arx.at[slot], across_x(offset, place))
-        for offset in sorted(range(nx), key=lambda o: -min(o, nx - o))
-        for place in (gy, other)
-        if not (place is gy and offset == 0)
-    ]
-
-    for copy in detail_copies:
-        copy.wait_recv()
-    detail_rows = [
-        send(da.at[:, :, 16:24, :], da.at[:, :, 0:8, :], other_core),
-        send(db.at[:, :, 16:24, :], db.at[:, :, 0:8, :], other_core),
-    ]
-
-    for copy in detail_rows:
-        copy.wait_recv()
+
+    @pl.when(gy == 0)
+    def _():
+        pl.semaphore_wait(mid, 4)
+        signal(link, other_core)
+
+    @pl.when(gy == 1)
+    def _():
+        pl.semaphore_wait(link, 1)
+
+    x_copies = send_all(
+        arx.at[0 : 2 * nx - 1],
+        *(
+            (row, arx.at[slot], across_x(offset, place))
+            for offset in sorted(range(nx), key=lambda o: -min(o, nx - o))
+            for place in (gy, other)
+            if not (place is gy and offset == 0)
+        ),
+    )
+
+    more_copies.wait_recv()
+    for k in range(5):
+        for half in range(2):
+            if k - half not in (1, 2):
+                level_one(k, half)
+
+    detail_rows = send_all(
+        db.at[:, :, 16:24, :], (db.at[:, :, 16:24, :], db.at[:, :, 0:8, :], other_core)
+    )
+    detail_rows.wait_recv()
 
     def along_z(t, carry):
         limit = thr[t]
         for part in range(3):
             rows = slice(8 * part, 8 * part + 8)
 
-            def cut(ref, band):
-                return [shrunk(ref[k, band, rows, :], limit) for k in range(5)]
-
-            pairs = (
-                (None, cut(da, 0)),
-                (cut(da, 1), cut(da, 2)),
-                (cut(db, 0), cut(db, 1)),
-                (cut(db, 2), cut(db, 3)),
-            )
+            def cut(band):
+                return [shrunk(db[k, band, rows, :], limit) for k in range(5)]
+
+            pairs = ((None, cut(0)), (cut(1), cut(2)), (cut(3), cut(4)), (cut(5), cut(6)))
             for band, (low, high) in enumerate(pairs):
                 for e in range(2):
                     order = [3 + e - i for i in range(4)]
@@ -345,18 +389,22 @@
 
     lax.fori_loop(0, 4, along_z, 0)
 
-    for copy in coeff_copies:
-        copy.wait_recv()
-    deep_rows = send(cb.at[:, :, :, 8:16, :], cb.at[:, :, :, 0:8, :], other_core)
-
-    for copy in x_copies:
-        copy.wait_recv()
+    coeff_copies.wait_recv()
+    deep_rows = send_all(
+        cb.at[:, :, :, 8:16, :],
+        (cb.at[:, :, :, 8:16, :], cb.at[:, :, :, 0:8, :], other_core),
+    )
+
+    x_copies.wait_recv()
     tot[...] = jnp.sum(arx[...], axis=0)
     arz[pl.ds(gz, 1)] = tot[...].reshape(1, 2, 128)
-    z_copies = [
-        send(tot, arz.at[gz], across_z(offset))
-        for offset in sorted(range(1, nz), key=lambda o: min(o, nz - o))
-    ]
+    z_copies = send_all(
+        arz.at[0 : nz - 1],
+        *(
+            (tot, arz.at[gz], across_z(offset))
+            for offset in sorted(range(1, nz), key=lambda o: min(o, nz - o))
+        ),
+    )
 
     deep_rows.wait_recv()
 
@@ -418,14 +466,13 @@
     both = jnp.concatenate([fo[0].reshape(512, 128), fo[1].reshape(512, 128)], axis=1)
     den[...] = product(both, a1t).reshape(4, 4, 32, 256)
 
-    for copy in z_copies:
-        copy.wait_recv()
+    z_copies.wait_recv()
     full = jnp.sum(arz[...], axis=0)
     cells = float(4 * 32 * 256 * total * 2)
     weights = jnp.where(lane[0:1] < 4, full[1:2], 1.0)
     gcv[...] = cells * full[0:1] / (weights * weights)
-    for copy in sent:
-        copy.wait_send()
+    for group in groups:
+        group.wait_send()
 
 
 def solution(mesh):
@@ -442,7 +489,6 @@
     second = analysis_matrix(128)
     forward = np.concatenate([first, first[:, 0:128] @ second], axis=1)
     matrices = [in_two_parts(m) for m in (forward, first.T, second.T)]
-    copies = 1 + 5 + 4 + 5 + 4 + (2 * nx - 1) + 2 + 1 + (nz - 1)
     f32 = jnp.float32
 
     def body(noisy_cube, thresholds):
@@ -461,12 +507,10 @@
                 pltpu.SMEM((4,), f32),
                 pltpu.VMEM((4, 56, 256), f32),
                 pltpu.VMEM((3, 4, 56, 128), f32),
-                pltpu.VMEM((10, 2, 16, 128), f32),
-                pltpu.VMEM((10, 2, 16, 128), f32),
+                pltpu.VMEM((16, 4, 16, 128), f32),
                 pltpu.VMEM((5, 2, 2, 8, 128), f32),
                 pltpu.VMEM((5, 2, 2, 8, 128), f32),
-                pltpu.VMEM((5, 3, 24, 128), f32),
-                pltpu.VMEM((5, 4, 24, 128), f32),
+                pltpu.VMEM((5, 7, 24, 128), f32),
                 pltpu.VMEM((6, 2, 2, 16, 128), f32),
                 pltpu.VMEM((4, 5, 2, 24, 128), f32),
                 pltpu.VMEM((4, 5, 32, 128), f32),
@@ -481,14 +525,16 @@
                 pltpu.VMEM((2 * nx, 2, 128), f32),
                 pltpu.VMEM((nz, 2, 128), f32),
                 pltpu.SemaphoreType.DMA((5,)),
-                pltpu.SemaphoreType.DMA((copies,)),
-                pltpu.SemaphoreType.DMA((copies,)),
-                pltpu.SemaphoreType.REGULAR((6,)),
+                pltpu.SemaphoreType.DMA((9,)),
+                pltpu.SemaphoreType.DMA((9,)),
+                pltpu.SemaphoreType.REGULAR,
+                pltpu.SemaphoreType.REGULAR,
+                pltpu.SemaphoreType.REGULAR,
             ],
             compiler_params=pltpu.CompilerParams(
                 collective_id=0, has_side_effects=True, vmem_limit_bytes=12 * 1024 * 1024
             ),
-        )(thresholds, noisy_cube, *(jnp.asarray(m) for m in matrices))
+        )(*(pltpu.with_memory_space_constraint(v, pltpu.HBM) for v in (thresholds, noisy_cube, *(jnp.asarray(m) for m in matrices))))
         return den, gcv[0, 0:4]
 
     return jax.shard_map(

time: 74.9 us -> 67.5 us (0.901)
  local copies, waits for them, and re-layouts: 5.64 us -> 1.31 us
  Pallas kernels: 68.4 us -> 65.4 us
    unnamed x11 -> x1, local copies, waits for them, and re-layouts: 5.13 us -> 0.79 us
    pallas_call x1, Pallas kernels: 68.4 us -> 65.4 us  [body(): pl.pallas_call(functools.partial(kernel, nx, nz), out_shape=(jax.ShapeDty...]
where the time goes in v3:
time: 67.5 us; the launch traced here: 67.3 us
  Pallas kernels  65.4 us (97%)
  local copies, waits for them, and re-layouts  1.31 us (2%)
    pallas_call x1, Pallas kernels, body(): pl.pallas_call(functools.partial(kernel, nx, nz), out_shape=(jax.ShapeDty...  65.4 us

profile of v3, /device:TPU:65, one launch (start us, length us, event | category | flops | bytes accessed | tf_op | source)
XLA Modules:
  0.0 67.3 jit_solution(5118969189992859960)
XLA Ops:
  0.6 65.4 %shard_map.68 = (f32[4,4,32,256]{3,2,1,0:T(8,128)S(1)}, f32[1,128]{1,0:T(1,128)S(1)}) custom-call(f32[4]{0:T(128)} %thr_hbm.1, f32[4,32,256]{2,1,0:T(8,128)} %x_hbm.1, bf16[2,256,384]{2,1,0:T(8,128)(2,1)} %constant.6.clone.a1_hbm, bf16[2,256,256]{2,1,0:T(8,128)(2,1)} %constant.7.clone.a1t_hbm, bf16[2,128,128]{2,1,0:T(8,128)(2,1)} %constant.8.clone.a2t_hbm), custom_call_target="tpu_custom_call" | custom-call | tf_op jit(solution)/shard_map/pallas_call | solution.py:495
  66.0 0.5 slice_bitcast_fusion
  66.5 0.8 %copy.8 = f32[4,4,32,256]{3,2,1,0:T(8,128)} copy(f32[4,4,32,256]{3,2,1,0:T(8,128)S(1)} %get-tuple-element.8) | data formatting | bytes 1048576

commit v4 on v3

--- a/solution.py
+++ b/solution.py
@@ -118,9 +118,9 @@
     other = 1 - gy
     other_core = (cube, gx, gz, other)
 
-    def along(offset):
+    def along(offset, core=None):
         place = lax.rem(flat + (offset + total), total)
-        return (cube, lax.div(place, nz), lax.rem(place, nz), gy)
+        return (cube, lax.div(place, nz), lax.rem(place, nz), gy if core is None else core)
 
     def across_x(offset, core):
         return (cube, lax.rem(gx + (offset + nx), nx), gz, core)
@@ -171,6 +171,9 @@
     def _():
         signal(barrier, other_core)
 
+    around = [along(offset, 0) for offset in (3, -3, 2, -2, 1, -1)]
+    signal(barrier, *around, across_x(1, 0), across_x(-1, 0))
+
     @pl.when(gy == 1)
     def _():
         pl.semaphore_wait(barrier, 1)
@@ -179,8 +182,6 @@
     @pl.when(gy == 0)
     def _():
         pl.semaphore_wait(link, 1)
-        signal(barrier, *(along(offset) for offset in (1, -1, 2, -2, 3, -3)))
-        signal(barrier, across_x(1, gy), across_x(-1, gy))
 
     loads[0].wait()
     rows_copy = send_all(
@@ -216,7 +217,7 @@
 
     @pl.when(gy == 0)
     def _():
-        pl.semaphore_wait(barrier, 8)
+        pl.semaphore_wait(barrier, 16)
         signal(link, other_core)
 
     @pl.when(gy == 1)
@@ -244,6 +245,11 @@
         (zw.at[8:10, 2:4], zw.at[4:6, 2:4], along(1)),
         (zw.at[6:8, 0:2], zw.at[10:12, 0:2], along(-1)),
     )
+    @pl.when(gy == 0)
+    def _():
+        signal(near, along(3), along(-3), across_x(1, gy), across_x(-1, gy))
+
+    plane_copies.wait_send()
     more_copies = send_all(
         six,
         (zw.at[8:10], zw.at[0:2], along(2)),
@@ -252,12 +258,6 @@
         (zw.at[8:10, 0:2], zw.at[12:14, 0:2], along(-1)),
     )
 
-    @pl.when(gy == 0)
-    def _():
-        signal(near, along(3), along(-3), across_x(1, gy), across_x(-1, gy))
-        pl.semaphore_wait(near, 4)
-        signal(mid, along(2), along(-2), across_x(2, gy), across_x(-2, gy))
-
     lane = lax.broadcasted_iota(jnp.int32, (8, 128), 1)
     first_half = lane < 64
     zero = jnp.zeros((8, 128), jnp.float32)
@@ -266,6 +266,12 @@
     squares = [limit * limit for limit in limits]
 
     part_copies.wait_recv()
+
+    @pl.when(gy == 0)
+    def _():
+        pl.semaphore_wait(near, 4)
+        signal(mid, along(2), along(-2), across_x(2, gy), across_x(-2, gy))
+
     residual = [zero] * 4
     weight = [zero] * 4
     for sz in range(2):
@@ -304,6 +310,12 @@
             db[k, 2 * band, 8:24, :] = weighted(HIGHPASS, planes)
 
     plane_copies.wait_recv()
+
+    @pl.when(gy == 0)
+    def _():
+        pl.semaphore_wait(mid, 4)
+        signal(link, other_core)
+
     for k in range(2):
         level_one(1 + k, 0)
         level_one(2 + k, 1)
@@ -337,11 +349,6 @@
     row[1:2, :] = as_row(sums[4:8])
     slot = gy * nx + gx
     arx[pl.ds(slot, 1)] = row[...].reshape(1, 2, 128)
-
-    @pl.when(gy == 0)
-    def _():
-        pl.semaphore_wait(mid, 4)
-        signal(link, other_core)
 
     @pl.when(gy == 1)
     def _():
@@ -470,9 +477,10 @@
     full = jnp.sum(arz[...], axis=0)
     cells = float(4 * 32 * 256 * total * 2)
     weights = jnp.where(lane[0:1] < 4, full[1:2], 1.0)
-    gcv[...] = cells * full[0:1] / (weights * weights)
+    gcv[...] = (cells * full[0:1] / (weights * weights))[:, 0:4]
     for group in groups:
-        group.wait_send()
+        if group is not plane_copies:
+            group.wait_send()
 
 
 def solution(mesh):
@@ -496,7 +504,7 @@
             functools.partial(kernel, nx, nz),
             out_shape=(
                 jax.ShapeDtypeStruct((4, 4, 32, 256), f32),
-                jax.ShapeDtypeStruct((1, 128), f32),
+                jax.ShapeDtypeStruct((1, 4), f32),
             ),
             in_specs=[pl.BlockSpec(memory_space=pltpu.HBM)] * 5,
             out_specs=(
@@ -535,7 +543,7 @@
                 collective_id=0, has_side_effects=True, vmem_limit_bytes=12 * 1024 * 1024
             ),
         )(*(pltpu.with_memory_space_constraint(v, pltpu.HBM) for v in (thresholds, noisy_cube, *(jnp.asarray(m) for m in matrices))))
-        return den, gcv[0, 0:4]
+        return den, gcv.reshape(4)
 
     return jax.shard_map(
         body,

time: 67.5 us -> 67.9 us (level)
  no operation moved by 1% of the time
where the time goes in v4:
time: 67.9 us; the launch traced here: 67.7 us
  Pallas kernels  65.8 us (97%)
  local copies, waits for them, and re-layouts  1.31 us (2%)
    pallas_call x1, Pallas kernels, body(): pl.pallas_call(functools.partial(kernel, nx, nz), out_shape=(jax.ShapeDty...  65.8 us

profile of v4, /device:TPU:65, one launch (start us, length us, event | category | flops | bytes accessed | tf_op | source)
XLA Modules:
  0.0 67.7 jit_solution(6123409298142395757)
XLA Ops:
  0.6 65.8 %shard_map.68 = (f32[4,4,32,256]{3,2,1,0:T(8,128)S(1)}, f32[1,4]{1,0:T(1,128)S(1)}) custom-call(f32[4]{0:T(128)} %thr_hbm.1, f32[4,32,256]{2,1,0:T(8,128)} %x_hbm.1, bf16[2,256,384]{2,1,0:T(8,128)(2,1)} %constant.6.clone.a1_hbm, bf16[2,256,256]{2,1,0:T(8,128)(2,1)} %constant.7.clone.a1t_hbm, bf16[2,128,128]{2,1,0:T(8,128)(2,1)} %constant.8.clone.a2t_hbm), custom_call_target="tpu_custom_call" | custom-call | tf_op jit(solution)/shard_map/pallas_call | solution.py:503
  66.4 0.8 %copy.9 = f32[4,4,32,256]{3,2,1,0:T(8,128)} copy(f32[4,4,32,256]{3,2,1,0:T(8,128)S(1)} %get-tuple-element.8) | data formatting | bytes 1048576
  67.2 0.5 copy.10

commit v5 on v4

--- a/solution.py
+++ b/solution.py
@@ -109,8 +109,10 @@
     send_sem,
     recv_sem,
     link,
-    near,
-    mid,
+    near_x,
+    mid_x,
+    near_z,
+    mid_z,
 ):
     cube, gx, gz, gy = (lax.axis_index(n) for n in ("cube", "gz_0", "gz_1", "gy"))
     total = nx * nz
@@ -126,7 +128,7 @@
         return (cube, lax.rem(gx + (offset + nx), nx), gz, core)
 
     def across_z(offset):
-        return (cube, gx, lax.rem(gz + offset, nz), gy)
+        return (cube, gx, lax.rem(gz + (offset + 2 * nz), nz), gy)
 
     groups = []
 
@@ -237,26 +239,22 @@
             taps = [xa[sx, z, pl.ds(j, 16, stride=2), :] for j in range(8)]
             zw[6 + z, sx] = weighted(LOWPASS, taps)
             zw[6 + z, 2 + sx] = weighted(HIGHPASS, taps)
-    six = zw.at[0:6]
     plane_copies = send_all(
-        six,
+        zw.at[0:6],
         (zw.at[6:10, 0:2], zw.at[2:6, 0:2], along(1)),
         (zw.at[6:10, 2:4], zw.at[10:14, 2:4], along(-1)),
         (zw.at[8:10, 2:4], zw.at[4:6, 2:4], along(1)),
         (zw.at[6:8, 0:2], zw.at[10:12, 0:2], along(-1)),
     )
-    @pl.when(gy == 0)
-    def _():
-        signal(near, along(3), along(-3), across_x(1, gy), across_x(-1, gy))
-
-    plane_copies.wait_send()
-    more_copies = send_all(
-        six,
-        (zw.at[8:10], zw.at[0:2], along(2)),
-        (zw.at[6:8], zw.at[14:16], along(-2)),
-        (zw.at[6:8, 2:4], zw.at[2:4, 2:4], along(1)),
-        (zw.at[8:10, 0:2], zw.at[12:14, 0:2], along(-1)),
-    )
+
+    @pl.when(gy == 0)
+    def _():
+        signal(near_x, across_x(1, gy), across_x(-1, gy))
+
+    @pl.when(gy == 0)
+    def _():
+        pl.semaphore_wait(near_x, 2)
+        signal(mid_x, across_x(2, gy), across_x(-2, gy))
 
     lane = lax.broadcasted_iota(jnp.int32, (8, 128), 1)
     first_half = lane < 64
@@ -266,12 +264,6 @@
     squares = [limit * limit for limit in limits]
 
     part_copies.wait_recv()
-
-    @pl.when(gy == 0)
-    def _():
-        pl.semaphore_wait(near, 4)
-        signal(mid, along(2), along(-2), across_x(2, gy), across_x(-2, gy))
-
     residual = [zero] * 4
     weight = [zero] * 4
     for sz in range(2):
@@ -309,13 +301,13 @@
                 db[k, 2 * band - 1, 8:24, :] = weighted(LOWPASS, planes)
             db[k, 2 * band, 8:24, :] = weighted(HIGHPASS, planes)
 
+    @pl.when(gy == 0)
+    def _():
+        pl.semaphore_wait(mid_x, 2)
+        signal(link, other_core)
+        signal(near_z, across_z(3), across_z(-3))
+
     plane_copies.wait_recv()
-
-    @pl.when(gy == 0)
-    def _():
-        pl.semaphore_wait(mid, 4)
-        signal(link, other_core)
-
     for k in range(2):
         level_one(1 + k, 0)
         level_one(2 + k, 1)
@@ -364,45 +356,30 @@
         ),
     )
 
-    more_copies.wait_recv()
-    for k in range(5):
-        for half in range(2):
-            if k - half not in (1, 2):
-                level_one(k, half)
-
-    detail_rows = send_all(
-        db.at[:, :, 16:24, :], (db.at[:, :, 16:24, :], db.at[:, :, 0:8, :], other_core)
-    )
-    detail_rows.wait_recv()
-
-    def along_z(t, carry):
-        limit = thr[t]
-        for part in range(3):
-            rows = slice(8 * part, 8 * part + 8)
-
-            def cut(band):
-                return [shrunk(db[k, band, rows, :], limit) for k in range(5)]
-
-            pairs = ((None, cut(0)), (cut(1), cut(2)), (cut(3), cut(4)), (cut(5), cut(6)))
-            for band, (low, high) in enumerate(pairs):
-                for e in range(2):
-                    order = [3 + e - i for i in range(4)]
-                    for odd in range(2):
-                        value = weighted(HIGHPASS[odd::2], [high[i] for i in order])
-                        if low is not None:
-                            value = value + weighted(LOWPASS[odd::2], [low[i] for i in order])
-                        zs1[2 * e + odd, t, band, rows, :] = value
-        return carry
-
-    lax.fori_loop(0, 4, along_z, 0)
-
-    coeff_copies.wait_recv()
-    deep_rows = send_all(
-        cb.at[:, :, :, 8:16, :],
-        (cb.at[:, :, :, 8:16, :], cb.at[:, :, :, 0:8, :], other_core),
-    )
+    detail_copies = send_all(
+        db.at[0:3, :, 8:24, :],
+        (db.at[2:4, 3:7, 8:24, :], db.at[0:2, 3:7, 8:24, :], along(1)),
+        (db.at[1:3, 0:3, 8:24, :], db.at[3:5, 0:3, 8:24, :], along(-1)),
+        (db.at[2, 0:3, 8:24, :], db.at[0, 0:3, 8:24, :], along(1)),
+        (db.at[2, 3:7, 8:24, :], db.at[4, 3:7, 8:24, :], along(-1)),
+    )
+
+    @pl.when(gy == 0)
+    def _():
+        pl.semaphore_wait(near_z, 2)
+        signal(mid_z, across_z(2), across_z(-2))
+
+    @pl.when(gy == 0)
+    def _():
+        pl.semaphore_wait(mid_z, 2)
+        signal(link, other_core)
 
     x_copies.wait_recv()
+
+    @pl.when(gy == 1)
+    def _():
+        pl.semaphore_wait(link, 1)
+
     tot[...] = jnp.sum(arx[...], axis=0)
     arz[pl.ds(gz, 1)] = tot[...].reshape(1, 2, 128)
     z_copies = send_all(
@@ -411,6 +388,17 @@
             (tot, arz.at[gz], across_z(offset))
             for offset in sorted(range(1, nz), key=lambda o: min(o, nz - o))
         ),
+    )
+
+    coeff_copies.wait_recv()
+    deep_rows = send_all(
+        cb.at[:, :, :, 8:16, :],
+        (cb.at[:, :, :, 8:16, :], cb.at[:, :, :, 0:8, :], other_core),
+    )
+
+    detail_copies.wait_recv()
+    detail_rows = send_all(
+        db.at[:, :, 16:24, :], (db.at[:, :, 16:24, :], db.at[:, :, 0:8, :], other_core)
     )
 
     deep_rows.wait_recv()
@@ -450,6 +438,29 @@
     loads[3].wait()
     cr[...] = product(co[:, :, 8:32, :].reshape(480, 128), a2t).reshape(4, 5, 24, 128)
 
+    detail_rows.wait_recv()
+
+    def along_z(t, carry):
+        limit = thr[t]
+        for part in range(3):
+            rows = slice(8 * part, 8 * part + 8)
+
+            def cut(band):
+                return [shrunk(db[k, band, rows, :], limit) for k in range(5)]
+
+            pairs = ((None, cut(0)), (cut(1), cut(2)), (cut(3), cut(4)), (cut(5), cut(6)))
+            for band, (low, high) in enumerate(pairs):
+                for e in range(2):
+                    order = [3 + e - i for i in range(4)]
+                    for odd in range(2):
+                        value = weighted(HIGHPASS[odd::2], [high[i] for i in order])
+                        if low is not None:
+                            value = value + weighted(LOWPASS[odd::2], [low[i] for i in order])
+                        zs1[2 * e + odd, t, band, rows, :] = value
+        return carry
+
+    lax.fori_loop(0, 4, along_z, 0)
+
     def along_y(t, carry):
         for part in range(3):
             rows = slice(8 * part, 8 * part + 8)
@@ -479,8 +490,7 @@
     weights = jnp.where(lane[0:1] < 4, full[1:2], 1.0)
     gcv[...] = (cells * full[0:1] / (weights * weights))[:, 0:4]
     for group in groups:
-        if group is not plane_copies:
-            group.wait_send()
+        group.wait_send()
 
 
 def solution(mesh):
@@ -538,6 +548,8 @@
                 pltpu.SemaphoreType.REGULAR,
                 pltpu.SemaphoreType.REGULAR,
                 pltpu.SemaphoreType.REGULAR,
+                pltpu.SemaphoreType.REGULAR,
+                pltpu.SemaphoreType.REGULAR,
             ],
             compiler_params=pltpu.CompilerParams(
                 collective_id=0, has_side_effects=True, vmem_limit_bytes=12 * 1024 * 1024

time: 67.9 us -> 67 us (0.987)
  Pallas kernels: 65.8 us -> 64.9 us
    pallas_call x1, Pallas kernels: 65.8 us -> 64.9 us  [body(): pl.pallas_call(functools.partial(kernel, nx, nz), out_shape=(jax.ShapeDty...]
where the time goes in v5:
time: 67 us; the launch traced here: 66.9 us
  Pallas kernels  64.9 us (97%)
  local copies, waits for them, and re-layouts  1.31 us (2%)
    pallas_call x1, Pallas kernels, body(): pl.pallas_call(functools.partial(kernel, nx, nz), out_shape=(jax.ShapeDty...  64.9 us

profile of v5, /device:TPU:65, one launch (start us, length us, event | category | flops | bytes accessed | tf_op | source)
XLA Modules:
  0.0 66.9 jit_solution(5711823151401101068)
XLA Ops:
  0.6 64.9 %shard_map.68 = (f32[4,4,32,256]{3,2,1,0:T(8,128)S(1)}, f32[1,4]{1,0:T(1,128)S(1)}) custom-call(f32[4]{0:T(128)} %thr_hbm.1, f32[4,32,256]{2,1,0:T(8,128)} %x_hbm.1, bf16[2,256,384]{2,1,0:T(8,128)(2,1)} %constant.6.clone.a1_hbm, bf16[2,256,256]{2,1,0:T(8,128)(2,1)} %constant.7.clone.a1t_hbm, bf16[2,128,128]{2,1,0:T(8,128)(2,1)} %constant.8.clone.a2t_hbm), custom_call_target="tpu_custom_call" | custom-call | tf_op jit(solution)/shard_map/pallas_call | solution.py:513
  65.5 0.8 %copy.9 = f32[4,4,32,256]{3,2,1,0:T(8,128)} copy(f32[4,4,32,256]{3,2,1,0:T(8,128)S(1)} %get-tuple-element.8) | data formatting | bytes 1048576
  66.3 0.5 copy.10

commit v6 on v5

--- a/solution.py
+++ b/solution.py
@@ -241,10 +241,10 @@
             zw[6 + z, 2 + sx] = weighted(HIGHPASS, taps)
     plane_copies = send_all(
         zw.at[0:6],
-        (zw.at[6:10, 0:2], zw.at[2:6, 0:2], along(1)),
-        (zw.at[6:10, 2:4], zw.at[10:14, 2:4], along(-1)),
-        (zw.at[8:10, 2:4], zw.at[4:6, 2:4], along(1)),
-        (zw.at[6:8, 0:2], zw.at[10:12, 0:2], along(-1)),
+        (zw.at[6:10, 0:3], zw.at[2:6, 0:3], along(1)),
+        (zw.at[6:8, 0:3], zw.at[10:12, 0:3], along(-1)),
+        (zw.at[6:10, 3], zw.at[10:14, 3], along(-1)),
+        (zw.at[8:10, 3], zw.at[4:6, 3], along(1)),
     )
 
     @pl.when(gy == 0)
@@ -293,13 +293,11 @@
                 residual[t] = residual[t] + cut
                 weight[t] = weight[t] + kept
 
-    def level_one(k, half):
-        for sx in range(2):
-            band = 2 * half + sx
-            planes = [zw[2 * k + j, band] for j in range(8)]
-            if band:
-                db[k, 2 * band - 1, 8:24, :] = weighted(LOWPASS, planes)
-            db[k, 2 * band, 8:24, :] = weighted(HIGHPASS, planes)
+    def level_one(k, band):
+        planes = [zw[2 * k + j, band] for j in range(8)]
+        if band:
+            db[k, 2 * band - 1, 8:24, :] = weighted(LOWPASS, planes)
+        db[k, 2 * band, 8:24, :] = weighted(HIGHPASS, planes)
 
     @pl.when(gy == 0)
     def _():
@@ -309,8 +307,9 @@
 
     plane_copies.wait_recv()
     for k in range(2):
-        level_one(1 + k, 0)
-        level_one(2 + k, 1)
+        for band in range(3):
+            level_one(1 + k, band)
+        level_one(2 + k, 3)
 
     def add_bands(first):
         def add_band(band, sums):
@@ -327,20 +326,16 @@
 
         return add_band
 
-    sums = lax.fori_loop(0, 3, add_bands(1), tuple(residual + weight))
-    sums = lax.fori_loop(3, 7, add_bands(2), sums)
-
-    def as_row(parts):
-        line = jnp.zeros((1, 128), jnp.float32)
-        for t, part in enumerate(parts):
-            value = jnp.sum(jnp.sum(part, axis=0, keepdims=True), axis=1, keepdims=True)
-            line = jnp.where(lane[0:1] == t, value, line)
-        return line
-
-    row[0:1, :] = as_row(sums[0:4])
-    row[1:2, :] = as_row(sums[4:8])
+    sums = lax.fori_loop(0, 5, add_bands(1), tuple(residual + weight))
+    sums = lax.fori_loop(5, 7, add_bands(2), sums)
+
+    line = jnp.zeros((1, 128), jnp.float32)
+    for index, part in enumerate(sums):
+        value = jnp.sum(jnp.sum(part, axis=0, keepdims=True), axis=1, keepdims=True)
+        line = jnp.where(lane[0:1] == index, value, line)
+    row[...] = line
     slot = gy * nx + gx
-    arx[pl.ds(slot, 1)] = row[...].reshape(1, 2, 128)
+    arx[pl.ds(slot, 1)] = row[...].reshape(1, 1, 128)
 
     @pl.when(gy == 1)
     def _():
@@ -358,10 +353,10 @@
 
     detail_copies = send_all(
         db.at[0:3, :, 8:24, :],
-        (db.at[2:4, 3:7, 8:24, :], db.at[0:2, 3:7, 8:24, :], along(1)),
-        (db.at[1:3, 0:3, 8:24, :], db.at[3:5, 0:3, 8:24, :], along(-1)),
-        (db.at[2, 0:3, 8:24, :], db.at[0, 0:3, 8:24, :], along(1)),
-        (db.at[2, 3:7, 8:24, :], db.at[4, 3:7, 8:24, :], along(-1)),
+        (db.at[1:3, 0:5, 8:24, :], db.at[3:5, 0:5, 8:24, :], along(-1)),
+        (db.at[2, 0:5, 8:24, :], db.at[0, 0:5, 8:24, :], along(1)),
+        (db.at[2:4, 5:7, 8:24, :], db.at[0:2, 5:7, 8:24, :], along(1)),
+        (db.at[2, 5:7, 8:24, :], db.at[4, 5:7, 8:24, :], along(-1)),
     )
 
     @pl.when(gy == 0)
@@ -381,7 +376,7 @@
         pl.semaphore_wait(link, 1)
 
     tot[...] = jnp.sum(arx[...], axis=0)
-    arz[pl.ds(gz, 1)] = tot[...].reshape(1, 2, 128)
+    arz[pl.ds(gz, 1)] = tot[...].reshape(1, 1, 128)
     z_copies = send_all(
         arz.at[0 : nz - 1],
         *(
@@ -487,8 +482,8 @@
     z_copies.wait_recv()
     full = jnp.sum(arz[...], axis=0)
     cells = float(4 * 32 * 256 * total * 2)
-    weights = jnp.where(lane[0:1] < 4, full[1:2], 1.0)
-    gcv[...] = (cells * full[0:1] / (weights * weights))[:, 0:4]
+    weights = full[:, 4:8]
+    gcv[...] = cells * full[:, 0:4] / (weights * weights)
     for group in groups:
         group.wait_send()
 
@@ -538,10 +533,10 @@
                 pltpu.VMEM((2, 256, 384), jnp.bfloat16),
                 pltpu.VMEM((2, 256, 256), jnp.bfloat16),
                 pltpu.VMEM((2, 128, 128), jnp.bfloat16),
-                pltpu.VMEM((2, 128), f32),
-                pltpu.VMEM((2, 128), f32),
-                pltpu.VMEM((2 * nx, 2, 128), f32),
-                pltpu.VMEM((nz, 2, 128), f32),
+                pltpu.VMEM((1, 128), f32),
+                pltpu.VMEM((1, 128), f32),
+                pltpu.VMEM((2 * nx, 1, 128), f32),
+                pltpu.VMEM((nz, 1, 128), f32),
                 pltpu.SemaphoreType.DMA((5,)),
                 pltpu.SemaphoreType.DMA((9,)),
                 pltpu.SemaphoreType.DMA((9,)),

time: 67 us -> 66.2 us (0.988)
  Pallas kernels: 64.9 us -> 64 us
    pallas_call x1, Pallas kernels: 64.9 us -> 64 us  [body(): pl.pallas_call(functools.partial(kernel, nx, nz), out_shape=(jax.ShapeDty...]
where the time goes in v6:
time: 66.2 us; the launch traced here: 66 us
  Pallas kernels  64 us (97%)
  local copies, waits for them, and re-layouts  1.31 us (2%)
    pallas_call x1, Pallas kernels, body(): pl.pallas_call(functools.partial(kernel, nx, nz), out_shape=(jax.ShapeDty...  64 us

profile of v6, /device:TPU:65, one launch (start us, length us, event | category | flops | bytes accessed | tf_op | source)
XLA Modules:
  0.0 66.0 jit_solution(16304653261511759758)
XLA Ops:
  0.6 64.0 %shard_map.68 = (f32[4,4,32,256]{3,2,1,0:T(8,128)S(1)}, f32[1,4]{1,0:T(1,128)S(1)}) custom-call(f32[4]{0:T(128)} %thr_hbm.1, f32[4,32,256]{2,1,0:T(8,128)} %x_hbm.1, bf16[2,256,384]{2,1,0:T(8,128)(2,1)} %constant.6.clone.a1_hbm, bf16[2,256,256]{2,1,0:T(8,128)(2,1)} %constant.7.clone.a1t_hbm, bf16[2,128,128]{2,1,0:T(8,128)(2,1)} %constant.8.clone.a2t_hbm), custom_call_target="tpu_custom_call" | custom-call | tf_op jit(solution)/shard_map/pallas_call | solution.py:508
  64.7 0.8 %copy.9 = f32[4,4,32,256]{3,2,1,0:T(8,128)} copy(f32[4,4,32,256]{3,2,1,0:T(8,128)S(1)} %get-tuple-element.8) | data formatting | bytes 1048576
  65.5 0.5 copy.10

commit v7 on v6

--- a/solution.py
+++ b/solution.py
@@ -241,10 +241,8 @@
             zw[6 + z, 2 + sx] = weighted(HIGHPASS, taps)
     plane_copies = send_all(
         zw.at[0:6],
-        (zw.at[6:10, 0:3], zw.at[2:6, 0:3], along(1)),
-        (zw.at[6:8, 0:3], zw.at[10:12, 0:3], along(-1)),
-        (zw.at[6:10, 3], zw.at[10:14, 3], along(-1)),
-        (zw.at[8:10, 3], zw.at[4:6, 3], along(1)),
+        (zw.at[6:10], zw.at[2:6], along(1)),
+        (zw.at[6:8], zw.at[10:12], along(-1)),
     )
 
     @pl.when(gy == 0)
@@ -307,27 +305,22 @@
 
     plane_copies.wait_recv()
     for k in range(2):
-        for band in range(3):
+        for band in range(4):
             level_one(1 + k, band)
-        level_one(2 + k, 3)
-
-    def add_bands(first):
-        def add_band(band, sums):
-            sums = list(sums)
-            for k in range(2):
-                for half in range(2):
-                    c = db[first + k, band, 8 + 8 * half : 16 + 8 * half, :]
-                    square = c * c
-                    for t in range(4):
-                        cut = jnp.clip(c, -limits[t], limits[t])
-                        sums[t] = sums[t] + cut * cut
-                        sums[4 + t] = sums[4 + t] + squares[t] / (squares[t] + square)
-            return tuple(sums)
-
-        return add_band
-
-    sums = lax.fori_loop(0, 5, add_bands(1), tuple(residual + weight))
-    sums = lax.fori_loop(5, 7, add_bands(2), sums)
+
+    def add_band(band, sums):
+        sums = list(sums)
+        for k in range(2):
+            for half in range(2):
+                c = db[1 + k, band, 8 + 8 * half : 16 + 8 * half, :]
+                square = c * c
+                for t in range(4):
+                    cut = jnp.clip(c, -limits[t], limits[t])
+                    sums[t] = sums[t] + cut * cut
+                    sums[4 + t] = sums[4 + t] + squares[t] / (squares[t] + square)
+        return tuple(sums)
+
+    sums = lax.fori_loop(0, 7, add_band, tuple(residual + weight))
 
     line = jnp.zeros((1, 128), jnp.float32)
     for index, part in enumerate(sums):
@@ -353,10 +346,8 @@
 
     detail_copies = send_all(
         db.at[0:3, :, 8:24, :],
-        (db.at[1:3, 0:5, 8:24, :], db.at[3:5, 0:5, 8:24, :], along(-1)),
-        (db.at[2, 0:5, 8:24, :], db.at[0, 0:5, 8:24, :], along(1)),
-        (db.at[2:4, 5:7, 8:24, :], db.at[0:2, 5:7, 8:24, :], along(1)),
-        (db.at[2, 5:7, 8:24, :], db.at[4, 5:7, 8:24, :], along(-1)),
+        (db.at[1:3, :, 8:24, :], db.at[3:5, :, 8:24, :], along(-1)),
+        (db.at[2, :, 8:24, :], db.at[0, :, 8:24, :], along(1)),
     )
 
     @pl.when(gy == 0)

time: 66.2 us -> 66.2 us (level)
  no operation moved by 1% of the time
where the time goes in v7:
time: 66.2 us; the launch traced here: 65.9 us
  Pallas kernels  64 us (97%)
  local copies, waits for them, and re-layouts  1.31 us (2%)
    pallas_call x1, Pallas kernels, body(): pl.pallas_call(functools.partial(kernel, nx, nz), out_shape=(jax.ShapeDty...  64 us

profile of v7, /device:TPU:65, one launch (start us, length us, event | category | flops | bytes accessed | tf_op | source)
XLA Modules:
  0.0 65.9 jit_solution(1757011850781287113)
XLA Ops:
  0.6 64.0 %shard_map.68 = (f32[4,4,32,256]{3,2,1,0:T(8,128)S(1)}, f32[1,4]{1,0:T(1,128)S(1)}) custom-call(f32[4]{0:T(128)} %thr_hbm.1, f32[4,32,256]{2,1,0:T(8,128)} %x_hbm.1, bf16[2,256,384]{2,1,0:T(8,128)(2,1)} %constant.6.clone.a1_hbm, bf16[2,256,256]{2,1,0:T(8,128)(2,1)} %constant.7.clone.a1t_hbm, bf16[2,128,128]{2,1,0:T(8,128)(2,1)} %constant.8.clone.a2t_hbm), custom_call_target="tpu_custom_call" | custom-call | tf_op jit(solution)/shard_map/pallas_call | solution.py:499
  64.6 0.8 %copy.9 = f32[4,4,32,256]{3,2,1,0:T(8,128)} copy(f32[4,4,32,256]{3,2,1,0:T(8,128)S(1)} %get-tuple-element.8) | data formatting | bytes 1048576
  65.4 0.5 copy.10

commit v8 on v7

--- a/solution.py
+++ b/solution.py
@@ -270,13 +270,6 @@
             for index in range(5):
                 c = c + part_in[index, sz, sy]
             cb[3, sz, sy, 8:16, :] = c
-    coeff_copies = send_all(
-        cb.at[0:5, :, :, 8:16, :],
-        *(
-            (cb.at[3, :, :, 8:16, :], cb.at[3 - offset, :, :, 8:16, :], along(offset))
-            for offset in (3, -2, 2, -1, 1)
-        ),
-    )
     for sz in range(2):
         for sy in range(2):
             c = cb[3, sz, sy, 8:16, :]
@@ -344,6 +337,13 @@
         ),
     )
 
+    coeff_copies = send_all(
+        cb.at[0:5, :, :, 8:16, :],
+        *(
+            (cb.at[3, :, :, 8:16, :], cb.at[3 - offset, :, :, 8:16, :], along(offset))
+            for offset in (3, -2, 2, -1, 1)
+        ),
+    )
     detail_copies = send_all(
         db.at[0:3, :, 8:24, :],
         (db.at[1:3, :, 8:24, :], db.at[3:5, :, 8:24, :], along(-1)),

time: 66.2 us -> 66.7 us (level)
  no operation moved by 1% of the time
where the time goes in v8:
time: 66.7 us; the launch traced here: 66.6 us
  Pallas kernels  64.6 us (97%)
  local copies, waits for them, and re-layouts  1.31 us (2%)
    pallas_call x1, Pallas kernels, body(): pl.pallas_call(functools.partial(kernel, nx, nz), out_shape=(jax.ShapeDty...  64.6 us

profile of v8, /device:TPU:65, one launch (start us, length us, event | category | flops | bytes accessed | tf_op | source)
XLA Modules:
  0.0 66.6 jit_solution(4044302368251052326)
XLA Ops:
  0.6 64.6 %shard_map.68 = (f32[4,4,32,256]{3,2,1,0:T(8,128)S(1)}, f32[1,4]{1,0:T(1,128)S(1)}) custom-call(f32[4]{0:T(128)} %thr_hbm.1, f32[4,32,256]{2,1,0:T(8,128)} %x_hbm.1, bf16[2,256,384]{2,1,0:T(8,128)(2,1)} %constant.6.clone.a1_hbm, bf16[2,256,256]{2,1,0:T(8,128)(2,1)} %constant.7.clone.a1t_hbm, bf16[2,128,128]{2,1,0:T(8,128)(2,1)} %constant.8.clone.a2t_hbm), custom_call_target="tpu_custom_call" | custom-call | tf_op jit(solution)/shard_map/pallas_call | solution.py:499
  65.3 0.8 %copy.9 = f32[4,4,32,256]{3,2,1,0:T(8,128)} copy(f32[4,4,32,256]{3,2,1,0:T(8,128)S(1)} %get-tuple-element.8) | data formatting | bytes 1048576
  66.1 0.5 copy.10
